TPU v7x, 32 devices: a whole 2x2x4 slice. The times are simulated.
32 devices in a mesh: dom: 8 (over z, x), feat: 4 (over y, core).
Axes of the slice: x: 2, y: 2, z: 4, core: 2. Of those that a mesh axis runs over, the one named last changes fastest.
Arguments:
- feats: bfloat16 [256, 4096], P('feat', 'dom'), may hold values from -6 to 6
- self_weight: bfloat16 [256, 256], P(None, 'feat'), may hold values from -0.375 to 0.375
- bases: bfloat16 [30, 256, 256], P(None, 'feat'), may hold values from -0.375 to 0.375
- coef: float32 [237, 30], replicated, may hold values from -1.2 to 1.2
- src_part: int32 [8192, 1], P('dom'), may hold values from 0 to 7; in each aligned block of 1024 rows (0 to 1023, 1024 to 2047, ...) at most 256 rows name the same one
- src_row: int32 [8192], P('dom'), may hold values from 0 to 511
- edge_dst: int32 [8192], P('dom'), may hold values from 0 to 511
- edge_rel: int32 [8192], P('dom'), may hold values from 0 to 236
- block_owner: int32 [64, 1], P('dom'), may hold values from 0 to 7; in each aligned block of 8 rows (0 to 7, 8 to 15, ...) at most 2 rows name the same one
- block_valid: int32 [8, 8], P('dom'), may hold values from 1 to 128, 896 in all within a row
- cotangent: bfloat16 [256, 4096], P('feat', 'dom'), may hold values from -6 to 6
Outputs:
- output: bfloat16 [256, 4096], P('feat', 'dom')
- grad_feats: bfloat16 [256, 4096], P('feat', 'dom')
- grad_bases: float32 [30, 256, 256], P(None, 'feat')
- grad_self: float32 [256, 256], P(None, 'feat')
- grad_coef: float32 [237, 30], replicated
Inputs may be any that keep to these rules, and one draw needn't show every extreme that they name: `src_part`: among the edge rows of one index of dom, no partition is the source partition of more than 256 rows, and some partition of exactly 256. `block_owner`: among the blocks of one index of dom, no partition owns more than 2, a bound that some block reaches. `block_valid`: the valid rows of a block come first; the counts of one index of dom sum to 896.
All inputs are finite; a program needn't handle non-finite values.
Results may differ from a plain program's by a relative error of at most 0.0055.
Values may be sent and summed in bfloat16 or wider, within the bound.
A program may use at most 64 MiB of HBM per device.

v0:
```python
import functools

import jax
import jax.numpy as jnp
from jax import lax
from jax.experimental import pallas as pl
from jax.experimental.pallas import tpu as pltpu
from jax.sharding import PartitionSpec as P

BF = jnp.bfloat16
F32 = jnp.float32


def dot(left, right, left_axis, right_axis):
    return lax.dot_general(
        left, right, (((left_axis,), (right_axis,)), ((), ())), preferred_element_type=F32
    )


def onehot(ids, start, size):
    return (jnp.arange(size, dtype=jnp.int32)[:, None] + start == ids[None, :]).astype(BF)


def spread(values, ids, width, chunk):
    if width <= chunk:
        return dot(values, onehot(ids, 0, width), 1, 1)

    def step(index, total):
        piece = dot(values, onehot(ids, index * chunk, chunk), 1, 1)
        return lax.dynamic_update_slice_in_dim(total, piece, index * chunk, 1)

    return lax.fori_loop(0, width // chunk, step, jnp.zeros((values.shape[0], width), F32))


def peers(axis, count):
    me = lax.axis_index(axis)
    return me, me // 2, me % 2, count // 2


def greet(groups):
    barrier = pltpu.get_barrier_semaphore()
    expected = 0
    for axis, count in groups:
        me, spot, side, columns = peers(axis, count)
        targets = [spot * 2 + 1 - side]
        targets += [(spot + hop) % columns * 2 + side for hop in range(1, columns)]
        for target in targets:
            pl.semaphore_signal(
                barrier, inc=1, device_id={axis: target}, device_id_type=pl.DeviceIdType.MESH
            )
        expected += columns
    pl.semaphore_wait(barrier, expected)


def remote(source, target_ref, send_sem, recv_sem, axis, target):
    return pltpu.make_async_remote_copy(
        src_ref=source,
        dst_ref=target_ref,
        send_sem=send_sem,
        recv_sem=recv_sem,
        device_id={axis: target},
        device_id_type=pl.DeviceIdType.MESH,
    )


class Gather:
    def __init__(self, axis, count, x_ref, o_ref, own_sem, send, recv, pair_send, pair_recv):
        self.me, self.spot, self.side, self.columns = peers(axis, count)
        self.axis, self.o_ref = axis, o_ref
        self.mate = self.spot * 2 + 1 - self.side
        self.pair_send, self.pair_recv = pair_send, pair_recv
        self.started, self.passed = [], []
        for hop in range(1, self.columns):
            target = (self.spot + hop) % self.columns * 2 + self.side
            copy = remote(
                x_ref, o_ref.at[self.me], send.at[hop - 1], recv.at[hop - 1], axis, target
            )
            copy.start()
            self.started.append(copy)
        first = remote(
            x_ref, o_ref.at[self.me], pair_send.at[0], pair_recv.at[0], axis, self.mate
        )
        first.start()
        self.passed.append(first)
        self.own = pltpu.make_async_copy(x_ref, o_ref.at[self.me], own_sem)
        self.own.start()

    def place(self, hop, side):
        return (self.spot - hop + self.columns) % self.columns * 2 + side

    def forward(self, hop):
        self.started[hop - 1].wait_recv()
        place = self.place(hop, self.side)
        copy = remote(
            self.o_ref.at[place],
            self.o_ref.at[place],
            self.pair_send.at[hop],
            self.pair_recv.at[hop],
            self.axis,
            self.mate,
        )
        copy.start()
        self.passed.append(copy)
        return place

    def from_mate(self, hop):
        self.passed[hop].wait_recv()
        return self.place(hop, 1 - self.side)

    def finish(self):
        for copy in self.started + self.passed:
            copy.wait_send()


def gather_scratch(count):
    columns = count // 2
    return [
        pltpu.SemaphoreType.DMA,
        pltpu.SemaphoreType.DMA((columns - 1,)),
        pltpu.SemaphoreType.DMA((columns - 1,)),
        pltpu.SemaphoreType.DMA((columns,)),
        pltpu.SemaphoreType.DMA((columns,)),
    ]


class Reduce:
    def __init__(
        self, axis, count, x_ref, landed, summed, arrived, send, recv, pair_send, pair_recv
    ):
        me, spot, side, columns = peers(axis, count)
        self.axis, self.side, self.columns, self.x_ref = axis, side, columns, x_ref
        self.landed, self.summed, self.arrived = landed, summed, arrived
        self.send, self.recv = send, recv
        self.order = [(spot + hop) % columns for hop in list(range(1, columns)) + [0]]
        self.passed, self.started = [], []
        for step, place in enumerate(self.order):
            copy = remote(
                x_ref.at[place * 2 + 1 - side],
                landed.at[step],
                pair_send.at[step],
                pair_recv.at[step],
                axis,
                spot * 2 + 1 - side,
            )
            copy.start()
            self.passed.append(copy)

    def middle(self, step):
        place = self.order[step]
        self.passed[step].wait_recv()
        total = self.x_ref[place * 2 + self.side].astype(F32) + self.landed[step].astype(F32)
        self.summed[step] = total.astype(BF)
        if step < self.columns - 1:
            copy = remote(
                self.summed.at[step],
                self.arrived.at[step],
                self.send.at[step],
                self.recv.at[step],
                self.axis,
                place * 2 + self.side,
            )
            copy.start()
            self.started.append(copy)

    def finish(self, o_ref):
        total = self.summed[self.columns - 1].astype(F32)
        for step, copy in enumerate(self.started):
            copy.wait_recv()
            total = total + self.arrived[step].astype(F32)
        o_ref[...] = total
        for copy in self.started + self.passed:
            copy.wait_send()


def reduce_scratch(count, shape):
    columns = count // 2
    return [
        pltpu.VMEM((columns,) + shape, BF),
        pltpu.VMEM((columns,) + shape, BF),
        pltpu.VMEM((columns - 1,) + shape, BF),
        pltpu.SemaphoreType.DMA((columns - 1,)),
        pltpu.SemaphoreType.DMA((columns - 1,)),
        pltpu.SemaphoreType.DMA((columns,)),
        pltpu.SemaphoreType.DMA((columns,)),
    ]


def exchange(kernel, out_shape, args, scratch, ident):
    vmem = pl.BlockSpec(memory_space=pltpu.VMEM)
    return pl.pallas_call(
        kernel,
        out_shape=out_shape,
        in_specs=[vmem] * len(args),
        out_specs=jax.tree.map(lambda leaf: vmem, out_shape),
        scratch_shapes=scratch,
        compiler_params=pltpu.CompilerParams(collective_id=ident, has_side_effects=True),
    )(*args)


def all_gather(values, axis, count, ident):
    def kernel(x_ref, o_ref, *scratch):
        greet([(axis, count)])
        gather = Gather(axis, count, x_ref, o_ref, *scratch)
        for hop in range(1, gather.columns):
            gather.forward(hop)
        gather.own.wait()
        for hop in range(gather.columns):
            gather.from_mate(hop)
        gather.finish()

    shape = jax.ShapeDtypeStruct((count,) + values.shape, values.dtype)
    return exchange(kernel, shape, (values,), gather_scratch(count), ident)


def gather_pick(values, ids, axis, count, ident):
    def kernel(x_ref, ids_ref, o_ref, table, total, *scratch):
        extent = x_ref.shape[1]
        greet([(axis, count)])
        gather = Gather(axis, count, x_ref, table, *scratch)
        rows = lax.broadcasted_iota(jnp.int32, (extent, ids_ref.shape[1]), 0)

        def use(place):
            hot = jnp.where(rows + place * extent == ids_ref[...], 1.0, 0.0).astype(BF)
            total[...] += jnp.dot(table[place], hot, preferred_element_type=F32)

        total[...] = jnp.zeros(total.shape, F32)
        gather.own.wait()
        use(gather.me)
        for hop in range(1, gather.columns):
            use(gather.forward(hop))
        for hop in range(gather.columns):
            use(gather.from_mate(hop))
        o_ref[...] = total[...].astype(BF)
        gather.finish()

    shape = (values.shape[0], ids.shape[1])
    scratch = [pltpu.VMEM((count,) + values.shape, BF), pltpu.VMEM(shape, F32)]
    return exchange(
        kernel,
        jax.ShapeDtypeStruct(shape, BF),
        (values, ids),
        scratch + gather_scratch(count),
        ident,
    )


def reduce_parts(values, axis, count, ident):
    def kernel(x_ref, o_ref, *scratch):
        greet([(axis, count)])
        reduce = Reduce(axis, count, x_ref, *scratch)
        for step in range(reduce.columns):
            reduce.middle(step)
        reduce.finish(o_ref)

    shape = values.shape[1:]
    return exchange(
        kernel, jax.ShapeDtypeStruct(shape, F32), (values,), reduce_scratch(count, shape), ident
    )


def reduce_both(first, axis, count, second, other_axis, other_count, ident):
    def kernel(x_ref, y_ref, o_ref, p_ref, *scratch):
        greet([(axis, count), (other_axis, other_count)])
        short = Reduce(axis, count, x_ref, *scratch[:7])
        long = Reduce(other_axis, other_count, y_ref, *scratch[7:])
        for step in range(short.columns):
            short.middle(step)
        for step in range(long.columns):
            long.middle(step)
        short.finish(o_ref)
        long.finish(p_ref)

    shape, other = first.shape[1:], second.shape[1:]
    return exchange(
        kernel,
        (jax.ShapeDtypeStruct(shape, F32), jax.ShapeDtypeStruct(other, F32)),
        (first, second),
        reduce_scratch(count, shape) + reduce_scratch(other_count, other),
        ident,
    )


def reduce_gather(values, pieces, axis, count, ident):
    def kernel(x_ref, y_ref, o_ref, p_ref, *scratch):
        greet([(axis, count)])
        reduce = Reduce(axis, count, x_ref, *scratch[:7])
        gather = Gather(axis, count, y_ref, p_ref, *scratch[7:])
        for step in range(reduce.columns):
            reduce.middle(step)
        for hop in range(1, gather.columns):
            gather.forward(hop)
        gather.own.wait()
        reduce.finish(o_ref)
        for hop in range(gather.columns):
            gather.from_mate(hop)
        gather.finish()

    shape = values.shape[1:]
    return exchange(
        kernel,
        (
            jax.ShapeDtypeStruct(shape, F32),
            jax.ShapeDtypeStruct((count,) + pieces.shape, pieces.dtype),
        ),
        (values, pieces),
        reduce_scratch(count, shape) + gather_scratch(count),
        ident,
    )


def by_part(values, count):
    rows, columns = values.shape
    return values.reshape(rows, count, columns // count).transpose(1, 0, 2)


def group_of(count):
    return max(size for size in range(1, 6) if count % size == 0)


def forward_kernel(group, bases_ref, sources_ref, weights_ref, out_ref):
    basis_count, quarter, width = bases_ref.shape
    sources = sources_ref[...]

    def step(index, total):
        part = bases_ref[pl.ds(index * group, group)].reshape(group * quarter, width)
        products = jnp.dot(part, sources, preferred_element_type=F32)
        for k in range(group):
            weight = weights_ref[pl.ds(index * group + k, 1), :]
            total = total + products[k * quarter:(k + 1) * quarter] * weight
        return total

    total = lax.fori_loop(0, basis_count // group, step, jnp.zeros(out_ref.shape, F32))
    out_ref[...] = total.astype(BF)


def backward_kernel(
    group, bases_ref, sources_ref, weights_ref, grad_ref, bases_out, scaled_out, edge_out
):
    basis_count, quarter, width = bases_ref.shape
    sources = sources_ref[...]
    edge_out[...] = jnp.zeros(edge_out.shape, F32)

    def step(index, carry):
        part = bases_ref[pl.ds(index * group, group)].reshape(group * quarter, width)
        products = jnp.dot(part, sources, preferred_element_type=F32)
        grad = grad_ref[...].astype(F32)
        combined = []
        for k in range(group):
            spot = pl.ds(index * group + k, 1)
            scaled_out[spot, :] = jnp.sum(
                products[k * quarter:(k + 1) * quarter] * grad, axis=0, keepdims=True
            )
            combined.append((grad * weights_ref[spot, :]).astype(BF))
        combined = jnp.concatenate(combined, axis=0)
        piece = dot(combined, sources, 1, 1)
        bases_out[pl.ds(index * group, group)] = piece.reshape(group, quarter, width).astype(BF)
        edge_out[...] += dot(part, combined, 0, 0)
        return carry

    lax.fori_loop(0, basis_count // group, step, 0)


def body(
    feats,
    self_weight,
    bases,
    coef,
    src_part,
    src_row,
    edge_dst,
    edge_rel,
    block_owner,
    block_valid,
    cotangent,
):
    dom_count = lax.axis_size("dom")
    feat_count = lax.axis_size("feat")
    quarter, entities = feats.shape
    edge_count = src_row.shape[0]
    block_count = block_valid.shape[1]
    block_rows = edge_count // block_count
    basis_count, _, width = bases.shape
    relations = coef.shape[0]
    total_entities = dom_count * entities
    chunk = min(8, dom_count) * entities
    scale = float(edge_count * dom_count) ** (-0.5)

    source_ids = src_part[:, 0] * entities + src_row
    live = (jnp.arange(block_rows)[None, :] < block_valid[0][:, None]).reshape(edge_count)
    owners = jnp.broadcast_to(block_owner, (block_count, block_rows)).reshape(edge_count)
    target_ids = jnp.where(live, owners * entities + edge_dst, -1)
    relation_hot = onehot(edge_rel, 0, relations)

    source_quarter = gather_pick(feats, source_ids[None, :], "dom", dom_count, 0)
    gathered = all_gather(
        jnp.concatenate([source_quarter, feats], axis=1), "feat", feat_count, 1
    ).reshape(width, edge_count + entities)
    sources = gathered[:, :edge_count]
    own_full = gathered[:, edge_count:]

    group = group_of(basis_count)
    vmem = pl.BlockSpec(memory_space=pltpu.VMEM)
    first = coef.astype(BF)
    second = (coef - first.astype(F32)).astype(BF)
    third = (coef - first.astype(F32) - second.astype(F32)).astype(BF)
    weights = (
        dot(first, relation_hot, 0, 0)
        + dot(second, relation_hot, 0, 0)
        + dot(third, relation_hot, 0, 0)
    )
    messages = pl.pallas_call(
        functools.partial(forward_kernel, group),
        out_shape=jax.ShapeDtypeStruct((quarter, edge_count), BF),
        in_specs=[vmem] * 3,
        out_specs=vmem,
    )(bases, sources, weights)
    extra = 16
    tail = jnp.zeros((extra, edge_count), BF).at[0].set(1.0)
    partial = spread(jnp.concatenate([messages, tail], axis=0), target_ids, total_entities, chunk)
    counted = partial[quarter:quarter + 1]
    high = jnp.floor(counted / 64.0)
    counts = jnp.concatenate(
        [high, counted - 64.0 * high, jnp.zeros((extra - 2, total_entities), F32)], axis=0
    )
    sent = jnp.concatenate([partial[:quarter], counts], axis=0).astype(BF)
    arrived = reduce_parts(by_part(sent, dom_count), "dom", dom_count, 2)
    aggregate = arrived[:quarter]
    degree = arrived[quarter:quarter + 1] * 64.0 + arrived[quarter + 1:quarter + 2]
    inverse_degree = 1.0 / jnp.maximum(degree, 1.0)
    preact = dot(self_weight, own_full, 0, 0) + inverse_degree * aggregate
    output = jax.nn.silu(preact).astype(BF)
    sigmoid_pre = jax.nn.sigmoid(preact)
    grad_pre = (
        cotangent.astype(F32) * sigmoid_pre * (1.0 + preact * (1.0 - sigmoid_pre))
    ).astype(BF)
    grad_node = (grad_pre.astype(F32) * inverse_degree).astype(BF)
    grad_message = gather_pick(grad_node, target_ids[None, :], "dom", dom_count, 3)

    grad_bases, scaled, edge_partial = pl.pallas_call(
        functools.partial(backward_kernel, group),
        out_shape=(
            jax.ShapeDtypeStruct((basis_count, quarter, width), BF),
            jax.ShapeDtypeStruct((basis_count, edge_count), F32),
            jax.ShapeDtypeStruct((width, edge_count), F32),
        ),
        in_specs=[vmem] * 4,
        out_specs=(vmem,) * 3,
    )(bases, sources, weights, grad_message)
    self_partial = dot(self_weight, grad_pre, 1, 0)
    self_term = dot(grad_pre, own_full, 1, 1)

    scaled_high = scaled.astype(BF)
    scaled_low = (scaled - scaled_high.astype(F32)).astype(BF)
    grad_coef = dot(scaled_high, relation_hot, 1, 1) + dot(scaled_low, relation_hot, 1, 1)
    lanes = -(-relations // 256) * 256
    coef_size = -(-basis_count // 32) * 32 * lanes
    coef_wide = coef_size // quarter
    padded = jnp.pad(
        grad_coef, ((0, coef_size // lanes - basis_count), (0, lanes - relations))
    ).reshape(quarter, coef_wide)
    both = jnp.concatenate([edge_partial, self_partial], axis=1).reshape(feat_count, quarter, -1)
    spare = jnp.broadcast_to(padded[None], (feat_count, quarter, coef_wide))
    both = jnp.concatenate([both, spare], axis=2).astype(BF)
    cut = basis_count * quarter
    more = -(cut + quarter) % (16 * dom_count)
    stacked = jnp.concatenate(
        [grad_bases.reshape(cut, width), self_term.astype(BF), jnp.zeros((more, width), BF)],
        axis=0,
    ).reshape(dom_count, -1, width)
    both, piece = reduce_both(both, "feat", feat_count, stacked, "dom", dom_count, 4)
    edge_grads = both[:, :edge_count].astype(BF)
    self_grads = both[:, edge_count:edge_count + entities]
    coef_sum = both[:, edge_count + entities:].reshape(-1, width)
    node_grads = by_part(
        spread(edge_grads, source_ids, total_entities, chunk).astype(BF), dom_count
    )
    height = piece.shape[0]
    pieces = (jnp.concatenate([piece, coef_sum], axis=0) * scale).astype(BF)
    node_sum, gathered = reduce_gather(node_grads, pieces, "dom", dom_count, 5)
    grad_feats = (self_grads + node_sum).astype(BF)
    whole = gathered[:, :height].reshape(-1, width).astype(F32)
    coef_total = jnp.sum(gathered[:, height:].astype(F32), axis=0)
    coef_total = coef_total.reshape(-1, lanes)[:basis_count, :relations].T
    return (
        output,
        grad_feats,
        whole[:cut].reshape(basis_count, quarter, width),
        whole[cut:cut + quarter].T,
        coef_total,
    )


def solution(mesh):
    return jax.shard_map(
        body,
        mesh=mesh,
        in_specs=(
            P("feat", "dom"),
            P(None, "feat"),
            P(None, "feat", None),
            P(),
            P("dom", None),
            P("dom"),
            P("dom"),
            P("dom"),
            P("dom", None),
            P("dom", None),
            P("feat", "dom"),
        ),
        out_specs=(P("feat", "dom"), P("feat", "dom"), P(None, "feat", None), P(None, "feat"), P()),
        check_vma=False,
    )
```

profile of v0, /device:TPU:0, one launch (start us, length us, event | category | flops | bytes accessed | tf_op | source)
XLA Modules:
  0.0 150.4 jit_solution(1946928633393800426)
XLA Ops:
  0.6 0.0 copy-start
  0.6 0.7 multiply_bitcast_fusion
  1.3 0.1 pad.19.clone
  1.4 0.8 fusion.29
  2.2 0.1 pad.11.clone
  2.2 0.7 broadcast_multiply_fusion
  2.9 1.3 add.36
  4.2 17.3 %shard_map.146 = bf16[64,1024]{1,0:T(8,128)(2,1)} custom-call(bf16[64,512]{1,0:T(8,128)(2,1)} %x_ref.1, s32[1,1024]{1,0:T(1,128)} %bitcast.71), custom_call_target="tpu_custom_call" | custom-call | tf_op jit(solution)/shard_map/pallas_call | solution.py:190
  21.5 1.6 %pad_maximum_fusion.2.x_ref = bf16[64,1536]{1,0:T(8,128)(2,1)} fusion(bf16[64,512]{1,0:T(8,128)(2,1)} %x_ref.1, bf16[64,1024]{1,0:T(8,128)(2,1)} %shard_map.146), kind=kLoop, calls=%fused_computation.39 | loop fusion | flops 393216 | bytes 393216 | tf_op jit(solution)/shard_map/concatenate | solution.py:396
  23.2 1.1 fusion.10
  24.3 1.1 fusion.11
  25.4 1.7 %fusion.7.weights_ref = f32[30,1024]{1,0:T(8,128)} fusion(f32[30,1024]{1,0:T(8,128)S(1)} %fusion.10, f32[30,1024]{1,0:T(8,128)S(1)} %fusion.11, s32[1024]{0:T(1024)} %param.20, f32[237,30]{0,1:T(8,128)} %param.16), kind=kOutput, calls=%fused_computation.12 | convolution fusion | flops 14872518 | bytes 401176 | tf_op jit(solution)/shard_map/dot_general | solution.py:15
  27.1 10.0 %shard_map.147 = bf16[4,64,1536]{2,1,0:T(8,128)(2,1)} custom-call(bf16[64,1536]{1,0:T(8,128)(2,1)} %pad_maximum_fusion.2.x_ref), custom_call_target="tpu_custom_call" | custom-call | tf_op jit(solution)/shard_map/pallas_call | solution.py:190
  37.2 1.9 %slice.77.sources_ref = bf16[256,1024]{1,0:T(8,128)(2,1)} slice(bf16[256,1536]{1,0:T(8,128)(2,1)} %bitcast.60), slice={[0:256], [0:1024]} | slice | bytes 1048576 | tf_op jit(solution)/shard_map/slice | solution.py:398
  39.1 4.2 %shard_map.148 = bf16[64,1024]{1,0:T(8,128)(2,1)} custom-call(bf16[30,64,256]{2,1,0:T(8,128)(2,1)} %bases_ref.3, bf16[256,1024]{1,0:T(8,128)(2,1)} %slice.77.sources_ref, f32[30,1024]{1,0:T(8,128)} %fusion.7.weights_ref), custom_call_target="tpu_custom_call" | custom-call | tf_op jit(solution)/shard_map/pallas_call | solution.py:411
  43.3 4.3 %fusion = f32[80,4096]{1,0:T(8,128)S(1)} fusion(s32[1024]{0:T(1024)S(1)} %fusion.29, bf16[16,1024]{1,0:T(8,128)(2,1)S(1)} %copy-done.8, bf16[64,1024]{1,0:T(8,128)(2,1)} %shard_map.148), kind=kOutput, calls=%fused_computation.2 | convolution fusion | flops 675610624 | bytes 1478656 | tf_op jit(solution)/shard_map/dot_general | solution.py:15
  47.6 0.1 slice.100
  47.7 0.0 copy-start.7
  47.7 1.1 maximum_bitcast_fusion.x_ref
  48.8 16.2 %shard_map.149 = f32[80,512]{1,0:T(8,128)} custom-call(bf16[8,80,512]{2,1,0:T(8,128)(2,1)} %maximum_bitcast_fusion.x_ref), custom_call_target="tpu_custom_call" | custom-call | tf_op jit(solution)/shard_map/pallas_call | solution.py:190
  65.0 0.8 maximum_divide_fusion
  65.9 1.8 %multiply_convert_fusion = (bf16[64,512]{1,0:T(8,128)(2,1)}, bf16[64,512]{1,0:T(8,128)(2,1)S(1)}, bf16[64,512]{1,0:T(8,128)(2,1)}) fusion(f32[512]{0:T(512)S(1)} %bitcast.74, bf16[64,512]{1,0:T(8,128)(2,1)S(1)} %copy-done.7, f32[80,512]{1,0:T(8,128)} %shard_map.149, bf16[256,64]{0,1:T(8,128)(2,1)S(1)} %copy-done, bf16[256,1536]{1,0:T(8,128)(2,1)S(1)} %bitcast.61), kind=kOutput, calls=%fused_computation.45 | convolution fusion | flops 17334272 | bytes 690176 | tf_op jit(solution)/shard_map/dot_general | solution.py:15
  67.7 0.2 convolution_convert_fusion.1
  67.9 14.5 %shard_map.150.grad_ref = bf16[64,1024]{1,0:T(8,128)(2,1)} custom-call(bf16[64,512]{1,0:T(8,128)(2,1)} %get-tuple-element.31.x_ref, s32[1,1024]{1,0:T(1,128)} %bitcast.72), custom_call_target="tpu_custom_call" | custom-call | tf_op jit(solution)/shard_map/pallas_call | solution.py:190
  82.4 0.3 fusion.5
  82.7 7.5 %shard_map.151 = (bf16[30,64,256]{2,1,0:T(8,128)(2,1)}, f32[30,1024]{1,0:T(8,128)}, f32[256,1024]{1,0:T(8,128)}) custom-call(bf16[30,64,256]{2,1,0:T(8,128)(2,1)} %bases_ref.3, bf16[256,1024]{1,0:T(8,128)(2,1)} %slice.77.sources_ref, f32[30,1024]{1,0:T(8,128)} %fusion.7.weights_ref, bf16[64,1024]{1,0:T(8,128)(2,1)} %shard_map.150.grad_ref), custom_call_target="tpu_custom_call" | custom-call | tf_op jit(solution)/shard_map/pallas_call | solution.py:439
  90.2 1.4 convert.35
  91.6 0.0 copy-start.5
  91.6 0.1 pad_maximum_fusion.1
  91.7 0.0 copy-done.2
  91.7 1.3 maximum_maximum_fusion
  93.0 0.3 fusion.9
  93.3 0.3 convolution_add_fusion
  93.6 0.0 copy-start.3
  93.6 1.0 pad_maximum_fusion.x_ref
  94.6 19.2 %shard_map.152 = (f32[64,1664]{1,0:T(8,128)}, f32[256,256]{1,0:T(8,128)}) custom-call(bf16[4,64,1664]{2,1,0:T(8,128)(2,1)} %pad_maximum_fusion.x_ref, bf16[8,256,256]{2,1,0:T(8,128)(2,1)} %bitcast.58), custom_call_target="tpu_custom_call" | custom-call | tf_op jit(solution)/shard_map/pallas_call | solution.py:190
  113.9 0.8 slice.70
  114.6 1.6 %fusion.17.y_ref = bf16[288,256]{1,0:T(8,128)(2,1)} fusion(f32[32,256]{1,0:T(8,128)S(1)} %reshape.86, f32[256,256]{1,0:T(8,128)} %get-tuple-element.28), kind=kLoop, calls=%fused_computation.34 | loop fusion | flops 221184 | bytes 442368 | tf_op jit(solution)/shard_map/convert_element_type | solution.py:478
  116.3 4.3 %fusion.4 = bf16[64,4096]{1,0:T(8,128)(2,1)S(1)} fusion(s32[1024]{0:T(1024)S(1)} %copy-done.3, f32[64,1664]{1,0:T(8,128)} %get-tuple-element.27), kind=kOutput, calls=%fused_computation.6 | convolution fusion | flops 541327360 | bytes 659456 | tf_op jit(solution)/shard_map/dot_general | solution.py:15
  120.6 0.8 copy.25
  121.4 22.2 %shard_map.153 = (f32[64,512]{1,0:T(8,128)}, bf16[8,288,256]{2,1,0:T(8,128)(2,1)}) custom-call(bf16[8,64,512]{2,1,0:T(8,128)(2,1)} %bitcast.64, bf16[288,256]{1,0:T(8,128)(2,1)} %fusion.17.y_ref), custom_call_target="tpu_custom_call" | custom-call | tf_op jit(solution)/shard_map/pallas_call | solution.py:190
  143.7 1.6 %add_convert_fusion = bf16[64,512]{1,0:T(8,128)(2,1)} fusion(f32[64,512]{1,0:T(8,128)} %get-tuple-element.29, f32[64,1664]{1,0:T(8,128)} %get-tuple-element.27), kind=kLoop, calls=%fused_computation.43 | loop fusion | flops 65536 | bytes 327680 | tf_op jit(solution)/shard_map/convert_element_type | solution.py:480
  145.3 0.9 convert_reduce_fusion
  146.2 1.3 slice.71
  147.5 0.6 slice_bitcast_fusion.1
  148.1 0.2 bitcast_convert_fusion
  148.4 0.6 slice_bitcast_fusion
  149.0 1.4 slice.81
  (21 shorter events, 0.1 us)
Async XLA Ops:
  0.6 65.2 %copy-start = (bf16[256,64]{0,1:T(8,128)(2,1)S(1)}, bf16[256,64]{0,1:T(8,128)(2,1)}, u32[]{:S(2)}) copy-start(bf16[256,64]{0,1:T(8,128)(2,1)} %param.14) | copy-start | bytes 98308
  2.2 41.1 %copy-start.4 = (s32[1024]{0:T(1024)}, s32[1024]{0:T(1024)S(1)}, u32[]{:S(2)}) copy-start(s32[1024]{0:T(1024)S(1)} %fusion.29) | copy-start | bytes 12292
  27.1 16.2 %copy-start.8 = (bf16[16,1024]{1,0:T(8,128)(2,1)S(1)}, bf16[16,1024]{1,0:T(8,128)(2,1)}, u32[]{:S(2)}) copy-start(bf16[16,1024]{1,0:T(8,128)(2,1)} %constant.48.clone.1) | copy-start | bytes 98308
  47.7 18.2 %copy-start.1 = (bf16[4,64,1536]{2,1,0:T(8,128)(2,1)S(1)}, bf16[4,64,1536]{2,1,0:T(8,128)(2,1)}, u32[]{:S(2)}) copy-start(bf16[4,64,1536]{2,1,0:T(8,128)(2,1)} %shard_map.147) | copy-start | bytes 2359300
  47.7 18.2 %copy-start.7 = (bf16[64,512]{1,0:T(8,128)(2,1)S(1)}, bf16[64,512]{1,0:T(8,128)(2,1)}, u32[]{:S(2)}) copy-start(bf16[64,512]{1,0:T(8,128)(2,1)} %param.23) | copy-start | bytes 196612
  90.2 1.5 %copy-start.2 = (bf16[30,64,256]{2,1,0:T(8,128)(2,1)S(1)}, bf16[30,64,256]{2,1,0:T(8,128)(2,1)}, u32[]{:S(2)}) copy-start(bf16[30,64,256]{2,1,0:T(8,128)(2,1)} %get-tuple-element.26) | copy-start | bytes 2949124
  91.6 1.4 copy-start.5
  91.6 1.4 copy-start.6
  93.6 22.6 %copy-start.3 = (s32[1024]{0:T(1024)S(1)}, s32[1024]{0:T(1024)}, u32[]{:S(2)}) copy-start(s32[1024]{0:T(1024)} %add.36) | copy-start | bytes 12292
where the time goes:
time: 153 us; the launch traced here: 150 us
  Pallas kernels  111 us (73%)
  matrix products  15.3 us (10%)
  other arithmetic  15.1 us (10%)
  local copies, waits for them, and re-layouts  7.84 us (5%)
    pallas_call x6, Pallas kernels, exchange(): pl.pallas_call(kernel, out_shape=out_shape, in_specs=[vmem] * len(args),...  99.6 us
    dot_general x10, matrix products, dot(): lax.dot_general(left, right, (((left_axis,), (right_axis,)), ((), ())), p...  15.3 us
    pallas_call x1, Pallas kernels, body(): pl.pallas_call(functools.partial(backward_kernel, group), out_shape=(jax....  7.51 us
    pallas_call x1, Pallas kernels, body(): pl.pallas_call(functools.partial(forward_kernel, group), out_shape=jax.Sh...  4.24 us

commit v1 on v0

v1 whole, which is shorter than its diff:
```python
from types import SimpleNamespace

import jax
import jax.numpy as jnp
from jax import lax
from jax.experimental import pallas as pl
from jax.experimental.pallas import tpu as pltpu
from jax.sharding import PartitionSpec as P

BF = jnp.bfloat16
F32 = jnp.float32
I32 = jnp.int32
LANES = 128
DOM, FEAT = "dom", "feat"


def dot(left, right, left_axis, right_axis):
    return lax.dot_general(
        left, right, (((left_axis,), (right_axis,)), ((), ())), preferred_element_type=F32
    )


def each(start, stop, step):
    if stop - start <= 8:
        for index in range(start, stop):
            step(index)
    else:
        lax.fori_loop(start, stop, lambda index, carry: (step(index), carry)[1], 0)


def peers(axis, count):
    me = lax.axis_index(axis)
    return me, me // 2, me % 2, count // 2


def greet(groups):
    barrier = pltpu.get_barrier_semaphore()
    for axis, count in groups:
        me = lax.axis_index(axis)

        def hello(hop):
            pl.semaphore_signal(
                barrier,
                inc=1,
                device_id={axis: (me + hop) % count},
                device_id_type=pl.DeviceIdType.MESH,
            )

        each(1, count, hello)
    return lambda: pl.semaphore_wait(barrier, sum(count - 1 for axis, count in groups))


def remote(source, target_ref, send_sem, recv_sem, axis, target):
    return pltpu.make_async_remote_copy(
        src_ref=source,
        dst_ref=target_ref,
        send_sem=send_sem,
        recv_sem=recv_sem,
        device_id={axis: target},
        device_id_type=pl.DeviceIdType.MESH,
    )


class Gather:
    def __init__(self, axis, count, source, table, sems):
        self.me, self.spot, self.side, self.columns = peers(axis, count)
        self.axis, self.source, self.table = axis, source, table
        self.sends, self.recvs, self.pair_sends, self.pair_recvs = sems

    def direct(self, hop):
        target = (self.spot + hop) % self.columns * 2 + self.side
        return remote(
            self.source,
            self.table(self.me),
            self.sends.at[hop - 1],
            self.recvs.at[hop - 1],
            self.axis,
            target,
        )

    def place(self, hop, side):
        return (self.spot - hop + self.columns) % self.columns * 2 + side

    def relay(self, hop, own=False):
        spot = self.table(self.place(hop, self.side))
        return remote(
            self.source if own else spot,
            spot,
            self.pair_sends.at[hop],
            self.pair_recvs.at[hop],
            self.axis,
            self.spot * 2 + 1 - self.side,
        )

    def start(self):
        each(1, self.columns, lambda hop: self.direct(hop).start())
        self.relay(0, True).start()

    def forward(self, hop):
        self.direct(hop).wait_recv()
        self.relay(hop).start()
        return self.place(hop, self.side)

    def from_mate(self, hop):
        self.relay(hop).wait_recv()
        return self.place(hop, 1 - self.side)

    def finish(self):
        each(1, self.columns, lambda hop: self.direct(hop).wait_send())
        each(0, self.columns, lambda hop: self.relay(hop).wait_send())


def gather_sems(count):
    columns = count // 2
    return [columns - 1, columns - 1, columns, columns]


class Swap:
    def __init__(self, axis, count, source, table, sems):
        self.me = lax.axis_index(axis)
        self.axis, self.count, self.source, self.table = axis, count, source, table
        self.sends, self.recvs = sems

    def copy(self, hop):
        target = (self.me + hop) % self.count
        return remote(
            self.source(target),
            self.table(self.me),
            self.sends.at[hop - 1],
            self.recvs.at[hop - 1],
            self.axis,
            target,
        )

    def start(self):
        each(1, self.count, lambda hop: self.copy(hop).start())

    def wait(self, hop):
        self.copy(hop).wait_recv()
        return (self.me - hop + self.count) % self.count

    def finish(self):
        each(1, self.count, lambda hop: self.copy(hop).wait_send())


def swap_sems(count):
    return [count - 1, count - 1]


class Reduce:
    def __init__(self, axis, count, block, landed, summed, arrived, sems):
        self.me, self.spot, self.side, self.columns = peers(axis, count)
        self.axis, self.block = axis, block
        self.landed, self.summed, self.arrived = landed, summed, arrived
        self.sends, self.recvs, self.pair_sends, self.pair_recvs = sems

    def place(self, step):
        return (self.spot + 1 + step) % self.columns

    def passing(self, step):
        return remote(
            self.block(self.place(step) * 2 + 1 - self.side),
            self.landed.at[step],
            self.pair_sends.at[step],
            self.pair_recvs.at[step],
            self.axis,
            self.spot * 2 + 1 - self.side,
        )

    def onward(self, step):
        return remote(
            self.summed.at[step],
            self.arrived.at[step],
            self.sends.at[step],
            self.recvs.at[step],
            self.axis,
            self.place(step) * 2 + self.side,
        )

    def pair(self, step):
        self.passing(step).wait_recv()
        own = self.block(self.place(step) * 2 + self.side)
        return own[...].astype(F32) + self.landed[step].astype(F32)

    def middle(self, step):
        self.summed[step] = self.pair(step).astype(BF)
        self.onward(step).start()

    def finish(self, total):
        total[...] = self.pair(self.columns - 1)

        def add(step):
            self.onward(step).wait_recv()
            total[...] += self.arrived[step].astype(F32)

        each(0, self.columns - 1, add)

    def drain(self):
        each(0, self.columns, lambda step: self.passing(step).wait_send())
        each(0, self.columns - 1, lambda step: self.onward(step).wait_send())


def sem_list(counts):
    return [pltpu.SemaphoreType.DMA((count,)) for count in counts]


def reduce_room(count, shape):
    columns = count // 2
    sizes = (columns, columns - 1, columns - 1)
    return [pltpu.VMEM((size,) + shape, BF) for size in sizes], sem_list(gather_sems(count))


def group_of(count):
    return max(size for size in range(1, 6) if count % size == 0)


def layer(
    feats, weight_t, bases, coef_t, part, row, dst, rel, cotangent, owner, valid, dom, feat
):
    quarter, entities = feats.shape
    width = weight_t.shape[1]
    edges = row.shape[1]
    blocks = valid.shape[1]
    rows = edges // blocks
    basis_count = bases.shape[0]
    relations = coef_t.shape[1]
    cap = max(1, 2 * blocks // dom)
    slots = cap * rows
    rel_pad = -(-relations // 256) * 256
    cut = basis_count * quarter
    total_rows = -(-(cut + quarter) // (16 * dom)) * 16 * dom
    while total_rows % quarter:
        total_rows += 16 * dom
    height = total_rows // dom
    basis_pad = total_rows // quarter
    rotated = height % quarter == 0
    group = height // quarter if rotated else group_of(basis_pad)
    basis_rows = -(-basis_count // 8) * 8
    while basis_rows * rel_pad // LANES % dom:
        basis_rows += 8
    coef_rows = basis_rows * rel_pad // LANES // dom
    chunks = 2
    span = edges // chunks
    scale = float(edges * dom) ** (-0.5)

    room = SimpleNamespace()
    room.bases = pltpu.VMEM((basis_pad, quarter, width), BF)
    room.bases_sems = sem_list([1])
    room.weights = pltpu.VMEM((basis_pad, edges), F32)
    room.rel_hot = pltpu.VMEM((rel_pad, edges), BF)
    room.coef_wide = pltpu.VMEM((basis_rows, rel_pad), F32)
    room.sids = pltpu.VMEM((1, edges), I32)
    room.tids = pltpu.VMEM((blocks, 1, rows), I32)
    room.slot_out = pltpu.VMEM((dom, cap, rows), I32)
    room.slot_in = pltpu.VMEM((dom, cap, rows), I32)
    room.slot_sems = sem_list(swap_sems(dom))
    room.hots = pltpu.VMEM((dom, entities, slots), BF)
    room.degree = pltpu.VMEM((16, entities), F32)
    room.table = pltpu.VMEM((dom, quarter, entities), BF)
    room.table_sems = sem_list(gather_sems(dom))
    room.picked = pltpu.VMEM((quarter, edges), F32)
    room.own = pltpu.VMEM((feat, quarter, entities), BF)
    room.own_sems = sem_list(gather_sems(feat))
    room.sources = pltpu.VMEM((feat, quarter, edges), BF)
    room.source_sems = [sem_list(gather_sems(feat)) for chunk in range(chunks)]
    room.products = pltpu.VMEM((total_rows, edges), BF)
    room.messages = pltpu.VMEM((blocks, quarter, rows), BF)
    room.message_out = pltpu.VMEM((dom, cap, quarter, rows), BF)
    room.message_in = pltpu.VMEM((dom, cap, quarter, rows), BF)
    room.message_sems = sem_list(swap_sems(dom))
    room.preact = pltpu.VMEM((quarter, entities), F32)
    room.aggregate = pltpu.VMEM((quarter, entities), F32)
    room.grad_out = pltpu.VMEM((dom, cap, quarter, rows), BF)
    room.grad_in = pltpu.VMEM((dom * cap, quarter, rows), BF)
    room.grad_sems = sem_list(swap_sems(dom))
    room.grad_message = pltpu.VMEM((quarter, edges), BF)
    room.self_rows = pltpu.VMEM((quarter, width), BF)
    room.self_send = pltpu.VMEM((feat, quarter, entities), BF)
    room.self_reduce = reduce_room(feat, (quarter, entities))
    room.self_sum = pltpu.VMEM((quarter, entities), F32)
    room.stack = pltpu.VMEM((total_rows, width), BF)
    room.stack_reduce = reduce_room(dom, (height, width))
    room.piece = pltpu.VMEM((height, width), F32)
    room.pieces_sems = sem_list(gather_sems(dom))
    room.scaled = pltpu.VMEM((basis_rows, edges), F32)
    room.combined = pltpu.VMEM(((2 if rotated else 1) * group * quarter, edges), BF)
    room.edge_sum = pltpu.VMEM((width, edges), F32)
    room.edge_send = pltpu.VMEM((feat, quarter, edges), BF)
    room.edge_reduce = reduce_room(feat, (quarter, edges))
    room.edge_total = pltpu.VMEM((quarter, edges), F32)
    room.edge_grad = pltpu.VMEM((quarter, edges), BF)
    room.nodes = pltpu.VMEM((dom, quarter, entities), BF)
    room.node_reduce = reduce_room(dom, (quarter, entities))
    room.node_sum = pltpu.VMEM((quarter, entities), F32)
    room.coef_out = pltpu.VMEM((dom, coef_rows, LANES), F32)
    room.coef_in = pltpu.VMEM((dom, coef_rows, LANES), F32)
    room.coef_sems = sem_list(swap_sems(dom))
    room.coef_feat = pltpu.VMEM((feat, coef_rows, LANES), F32)
    room.coef_feat_sems = sem_list(swap_sems(feat))
    room.coef_all_sems = sem_list(swap_sems(dom))

    shapes, tree = jax.tree.flatten(vars(room))

    def kernel(
        feats_ref,
        weight_ref,
        bases_hbm,
        coef_ref,
        part_ref,
        row_ref,
        dst_ref,
        rel_ref,
        cot_ref,
        owner_ref,
        valid_ref,
        output_ref,
        grad_feats_ref,
        pieces_ref,
        coef_all_ref,
        *scratch,
    ):
        at = SimpleNamespace(**jax.tree.unflatten(tree, scratch))

        def reduce_of(space, axis, count, block):
            buffers, sems = space
            return Reduce(axis, count, block, *buffers, sems)

        me = lax.axis_index(DOM)
        fme = lax.axis_index(FEAT)
        met = greet([(DOM, dom), (FEAT, feat)])

        load = pltpu.make_async_copy(
            bases_hbm, at.bases.at[pl.ds(0, basis_count)], at.bases_sems[0].at[0]
        )
        load.start()
        if basis_pad > basis_count:
            extra = basis_pad - basis_count
            at.bases[basis_count:] = jnp.zeros((extra, quarter, width), BF)
        at.sids[...] = part_ref[...] * entities + row_ref[...]
        lane = lax.broadcasted_iota(I32, (1, rows), 1)
        spots = []
        for k in range(blocks):
            ids = dst_ref[:, k * rows:(k + 1) * rows]
            at.tids[k] = jnp.where(lane < valid_ref[0, k], ids, -1)
            rank = 0
            for other in range(k):
                rank = rank + jnp.where(owner_ref[0, other] == owner_ref[0, k], 1, 0)
            spots.append(owner_ref[0, k] * cap + rank)

        def block_at(slot):
            found = -1
            for k in range(blocks):
                found = jnp.where(spots[k] == slot, k, found)
            return found

        def fill(place):
            for j in range(cap):
                found = block_at(place * cap + j)
                used = jnp.where(found >= 0, 1, 0)
                ids = at.tids[jnp.maximum(found, 0)]
                at.slot_out[place, j:j + 1] = ids * used + (used - 1)

        each(0, dom, fill)
        at.slot_in[me] = at.slot_out[me]

        at.coef_wide[...] = jnp.zeros((basis_rows, rel_pad), F32)
        at.coef_wide[:basis_count, :relations] = coef_ref[...]
        wide = at.coef_wide[...]
        first = wide.astype(BF)
        second = (wide - first.astype(F32)).astype(BF)
        third = (wide - first.astype(F32) - second.astype(F32)).astype(BF)
        thirds = jnp.concatenate([first, second, third], axis=0)
        rel_rows = lax.broadcasted_iota(I32, (rel_pad, rows), 0)
        for k in range(blocks):
            lanes = slice(k * rows, (k + 1) * rows)
            at.rel_hot[:, lanes] = jnp.where(rel_rows == rel_ref[:, lanes], 1.0, 0.0).astype(BF)
        three = dot(thirds, at.rel_hot[...], 1, 0)
        weights = three[:basis_rows] + three[basis_rows:2 * basis_rows] + three[2 * basis_rows:]
        if basis_pad <= basis_rows:
            at.weights[...] = weights[:basis_pad]
        else:
            at.weights[:basis_rows] = weights
            at.weights[basis_rows:] = jnp.zeros((basis_pad - basis_rows, edges), F32)
        at.own[fme] = feats_ref[...]

        met()

        table = Gather(
            DOM, dom, feats_ref, lambda place: at.table.at[place], at.table_sems
        )
        slot = Swap(
            DOM,
            dom,
            lambda place: at.slot_out.at[place],
            lambda place: at.slot_in.at[place],
            at.slot_sems,
        )
        slot.start()
        table.start()
        own = Gather(
            FEAT,
            feat,
            at.own.at[fme],
            lambda place: at.own.at[place],
            at.own_sems,
        )
        own.start()

        entity_rows = lax.broadcasted_iota(I32, (entities, edges), 0)

        def hot_of(place):
            hot = entity_rows + place * entities == at.sids[...]
            return jnp.where(hot, 1.0, 0.0).astype(BF)

        def use(place):
            at.picked[...] += dot(at.table[place], hot_of(place), 1, 0)

        at.picked[...] = dot(feats_ref[...], hot_of(me), 1, 0)
        use(table.from_mate(0))
        each(1, own.columns, lambda hop: own.forward(hop))
        each(1, table.columns, lambda hop: use(table.forward(hop)))
        each(1, table.columns, lambda hop: use(table.from_mate(hop)))

        gathers = []
        for chunk in range(chunks):
            lanes = pl.ds(chunk * span, span)
            at.sources[fme, :, lanes] = at.picked[:, lanes].astype(BF)
            gather = Gather(
                FEAT,
                feat,
                at.sources.at[fme, :, lanes],
                lambda place, lanes=lanes: at.sources.at[place, :, lanes],
                at.source_sems[chunk],
            )
            gather.start()
            gathers.append(gather)
        each(0, own.columns, lambda hop: own.from_mate(hop))
        own_full = at.own[...].reshape(width, entities)
        at.preact[...] = dot(weight_ref[...], own_full, 1, 0)
        load.wait()

        def forward(chunk):
            lanes = pl.ds(chunk * span, span)
            sources = at.sources[:, :, lanes].reshape(width, span)
            products = dot(at.bases[...].reshape(total_rows, width), sources, 1, 0)
            at.products[:, lanes] = products.astype(BF)
            total = jnp.zeros((quarter, span), F32)
            for k in range(basis_count):
                total += products[k * quarter:(k + 1) * quarter] * at.weights[k:k + 1, lanes]
            total = total.astype(BF)
            for k in range(span // rows):
                at.messages[chunk * (span // rows) + k] = total[:, k * rows:(k + 1) * rows]

        for gather in gathers:
            each(1, gather.columns, lambda hop: gather.forward(hop))
        for chunk, gather in enumerate(gathers):
            each(0, gather.columns, lambda hop: gather.from_mate(hop))
            forward(chunk)

        message = Swap(
            DOM,
            dom,
            lambda place: at.message_out.at[place],
            lambda place: at.message_in.at[place],
            at.message_sems,
        )

        def load_out(place):
            for j in range(cap):
                found = jnp.maximum(block_at(place * cap + j), 0)
                at.message_out[place, j] = at.messages[found]

        def send_out(hop):
            load_out((me + hop) % dom)
            message.copy(hop).start()

        each(1, dom, send_out)
        load_out(me)
        at.message_in[me] = at.message_out[me]

        slot_rows = lax.broadcasted_iota(I32, (entities, rows), 0)
        ones = jnp.ones((16, slots), BF)

        def slot_hot(place):
            parts = [
                jnp.where(slot_rows == at.slot_in[place, j:j + 1], 1.0, 0.0).astype(BF)
                for j in range(cap)
            ]
            hot = jnp.concatenate(parts, axis=1)
            at.hots[place] = hot
            at.degree[...] += dot(ones, hot, 1, 1)

        at.degree[...] = jnp.zeros((16, entities), F32)
        slot_hot(me)
        each(1, dom, lambda hop: slot_hot(slot.wait(hop)))

        def gather_in(place):
            parts = [at.message_in[place, j] for j in range(cap)]
            value = jnp.concatenate(parts, axis=1)
            return dot(value, at.hots[place], 1, 1)

        at.aggregate[...] = gather_in(me)

        def take(hop):
            at.aggregate[...] += gather_in(message.wait(hop))

        each(1, dom, take)

        inverse = 1.0 / jnp.maximum(at.degree[0:1, :], 1.0)
        preact = at.preact[...] + inverse * at.aggregate[...]
        sigmoid = jax.nn.sigmoid(preact)
        output_ref[...] = (preact * sigmoid).astype(BF)
        grad_pre = (cot_ref[...].astype(F32) * sigmoid * (1.0 + preact * (1.0 - sigmoid))).astype(BF)
        grad_node = (grad_pre.astype(F32) * inverse).astype(BF)

        back = Swap(
            DOM,
            dom,
            lambda place: at.grad_out.at[place],
            lambda place: at.grad_in.at[pl.ds(place * cap, cap)],
            at.grad_sems,
        )

        def slot_grads(place, target):
            value = dot(grad_node, at.hots[place], 1, 0).astype(BF)
            for j in range(cap):
                target[j] = value[:, j * rows:(j + 1) * rows]

        def send_back(hop):
            place = (me + hop) % dom
            slot_grads(place, at.grad_out.at[place])
            back.copy(hop).start()

        each(1, dom, send_back)
        slot_grads(me, at.grad_in.at[pl.ds(me * cap, cap)])

        own_full = at.own[...].reshape(width, entities)
        at.self_rows[...] = dot(grad_pre, own_full, 1, 1).astype(BF)
        at.self_send[...] = (
            dot(weight_ref[...], grad_pre, 0, 0).astype(BF).reshape(feat, quarter, entities)
        )
        self_reduce = reduce_of(at.self_reduce, FEAT, feat, lambda place: at.self_send.at[place])
        each(0, self_reduce.columns, lambda step: self_reduce.passing(step).start())
        at.edge_sum[...] = jnp.zeros((width, edges), F32)

        each(1, dom, lambda hop: back.wait(hop))
        for k in range(blocks):
            at.grad_message[:, k * rows:(k + 1) * rows] = at.grad_in[spots[k]]

        def combine(base, half):
            for chunk in range(chunks):
                lanes = pl.ds(chunk * span, span)
                grad = at.grad_message[:, lanes].astype(F32)
                for k in range(group):
                    weight = at.weights[pl.ds(base + k, 1), lanes]
                    top = (half * group + k) * quarter
                    at.combined[top:top + quarter, lanes] = (grad * weight).astype(BF)
            block = at.combined[half * group * quarter:(half + 1) * group * quarter, :]
            piece = dot(block, at.sources[...].reshape(width, edges), 1, 1)
            start = pl.multiple_of(base * quarter, group * quarter)
            at.stack[pl.ds(start, group * quarter), :] = piece.astype(BF)

            @pl.when(base + group == basis_pad)
            def _():
                at.stack[cut:cut + quarter, :] = at.self_rows[...]

        def part_of(base):
            return at.bases[pl.ds(base, group)].reshape(group * quarter, width)

        def edge_add(parts):
            count = len(parts) * group * quarter
            value = jnp.concatenate(parts, axis=0)
            at.edge_sum[...] += dot(value, at.combined[:count, :], 0, 0)

        stack = reduce_of(
            at.stack_reduce,
            DOM,
            dom,
            lambda place: at.stack.at[pl.ds(pl.multiple_of(place * height, height), height)],
        )
        if rotated:

            def work(step):
                place = stack.place(step)
                other = (place * 2 + 1 - stack.side) * group
                mine = (place * 2 + stack.side) * group
                combine(other, 0)
                stack.passing(step).start()
                combine(mine, 1)
                edge_add([part_of(other), part_of(mine)])

            each(0, stack.columns, work)
        else:

            def whole(index, carry):
                combine(index * group, 0)
                edge_add([part_of(index * group)])
                return carry

            lax.fori_loop(0, basis_pad // group, whole, 0)
            each(0, stack.columns, lambda step: stack.passing(step).start())

        edge = reduce_of(at.edge_reduce, FEAT, feat, lambda place: at.edge_send.at[place])
        at.edge_send[...] = at.edge_sum[...].astype(BF).reshape(feat, quarter, edges)
        each(0, edge.columns, lambda step: edge.passing(step).start())
        each(0, self_reduce.columns - 1, self_reduce.middle)
        ahead = min(1, stack.columns - 1)
        each(0, ahead, stack.middle)
        each(0, edge.columns - 1, edge.middle)

        at.scaled[...] = jnp.zeros((basis_rows, edges), F32)
        for chunk in range(chunks):
            lanes = pl.ds(chunk * span, span)
            grad = at.grad_message[:, lanes].astype(F32)
            for k in range(basis_count):
                value = at.products[k * quarter:(k + 1) * quarter, lanes].astype(F32) * grad
                at.scaled[k:k + 1, lanes] = jnp.sum(value, axis=0, keepdims=True)
        scaled = at.scaled[...]
        high = scaled.astype(BF)
        low = (scaled - high.astype(F32)).astype(BF)
        both = dot(jnp.concatenate([high, low], axis=0), at.rel_hot[...], 1, 1)
        coef_part = (both[:basis_rows] + both[basis_rows:]) * scale
        tall = jnp.concatenate(
            [coef_part[:, k * LANES:(k + 1) * LANES] for k in range(rel_pad // LANES)], axis=0
        )
        at.coef_out[...] = tall.reshape(dom, coef_rows, LANES)
        coef = Swap(
            DOM,
            dom,
            lambda place: at.coef_out.at[place],
            lambda place: at.coef_in.at[place],
            at.coef_sems,
        )
        coef.start()
        at.coef_in[me] = at.coef_out[me]
        each(ahead, stack.columns - 1, stack.middle)

        self_reduce.finish(at.self_sum)
        edge.finish(at.edge_total)
        at.edge_grad[...] = at.edge_total[...].astype(BF)
        node = reduce_of(at.node_reduce, DOM, dom, lambda place: at.nodes.at[place])

        def scatter(place):
            at.nodes[place] = dot(at.edge_grad[...], hot_of(place), 1, 1).astype(BF)

        def spread(step):
            place = node.place(step)
            scatter(place * 2 + 1 - node.side)
            node.passing(step).start()
            scatter(place * 2 + node.side)

        half = node.columns // 2
        each(0, half, spread)
        each(1, dom, lambda hop: coef.wait(hop))
        at.coef_feat[fme] = jnp.sum(at.coef_in[...], axis=0)
        coef_feat = Swap(
            FEAT,
            feat,
            lambda place: at.coef_feat.at[fme],
            lambda place: at.coef_feat.at[place],
            at.coef_feat_sems,
        )
        coef_feat.start()
        each(half, node.columns, spread)
        each(1, feat, lambda hop: coef_feat.wait(hop))
        coef_all_ref[me] = jnp.sum(at.coef_feat[...], axis=0)
        coef_all = Swap(
            DOM,
            dom,
            lambda place: coef_all_ref.at[me],
            lambda place: coef_all_ref.at[place],
            at.coef_all_sems,
        )
        coef_all.start()

        stack.finish(at.piece)
        pieces_ref[me] = (at.piece[...] * scale).astype(BF)
        pieces = Gather(
            DOM, dom, pieces_ref.at[me], lambda place: pieces_ref.at[place], at.pieces_sems
        )
        pieces.start()
        each(0, node.columns - 1, node.middle)
        each(1, pieces.columns, lambda hop: pieces.forward(hop))
        node.finish(at.node_sum)
        grad_feats_ref[...] = (at.self_sum[...] + at.node_sum[...]).astype(BF)
        each(0, pieces.columns, lambda hop: pieces.from_mate(hop))
        each(1, dom, lambda hop: coef_all.wait(hop))

        for done in [table, slot, own, message, back, coef, coef_feat, coef_all, pieces] + gathers:
            done.finish()
        for done in [self_reduce, stack, edge, node]:
            done.drain()

    vmem = pl.BlockSpec(memory_space=pltpu.VMEM)
    smem = pl.BlockSpec(memory_space=pltpu.SMEM)
    output, grad_feats, pieces, coef_all = pl.pallas_call(
        kernel,
        out_shape=(
            jax.ShapeDtypeStruct((quarter, entities), BF),
            jax.ShapeDtypeStruct((quarter, entities), BF),
            jax.ShapeDtypeStruct((dom, height, width), BF),
            jax.ShapeDtypeStruct((dom, coef_rows, LANES), F32),
        ),
        in_specs=[vmem, vmem, pl.BlockSpec(memory_space=pl.ANY)] + [vmem] * 6 + [smem] * 2,
        out_specs=(vmem,) * 4,
        scratch_shapes=shapes,
        compiler_params=pltpu.CompilerParams(
            collective_id=0, has_side_effects=True, vmem_limit_bytes=60 * 1024 * 1024
        ),
    )(feats, weight_t, bases, coef_t, part, row, dst, rel, cotangent, owner, valid)

    step = group_of(basis_count)
    halves = rel_pad // LANES

    def last(output_in, feats_in, bases_in, self_in, coef_in, *outs):
        outs[2][...] = bases_in[...].astype(F32).reshape(step, quarter, width)

        @pl.when(pl.program_id(0) == 0)
        def _():
            outs[0][...] = output_in[...]
            outs[1][...] = feats_in[...]
            outs[3][...] = self_in[...].astype(F32)
            parts = [coef_in[k * basis_rows:(k + 1) * basis_rows] for k in range(halves)]
            outs[4][...] = jnp.concatenate(parts, axis=1)[:basis_count, :relations]

    flat = pieces.reshape(total_rows, width)

    def fixed(shape, spot=0):
        return pl.BlockSpec(shape, lambda index: (spot,) + (0,) * (len(shape) - 1))

    output, grad_feats, grad_bases, grad_self, grad_coef = pl.pallas_call(
        last,
        grid=(basis_count // step,),
        out_shape=(
            jax.ShapeDtypeStruct((quarter, entities), BF),
            jax.ShapeDtypeStruct((quarter, entities), BF),
            jax.ShapeDtypeStruct((basis_count, quarter, width), F32),
            jax.ShapeDtypeStruct((quarter, width), F32),
            jax.ShapeDtypeStruct((basis_count, relations), F32),
        ),
        in_specs=[
            fixed((quarter, entities)),
            fixed((quarter, entities)),
            pl.BlockSpec((step * quarter, width), lambda index: (index, 0)),
            fixed((quarter, width), cut // quarter),
            fixed((halves * basis_rows, LANES)),
        ],
        out_specs=(
            fixed((quarter, entities)),
            fixed((quarter, entities)),
            pl.BlockSpec((step, quarter, width), lambda index: (index, 0, 0)),
            fixed((quarter, width)),
            fixed((basis_count, relations)),
        ),
    )(output, grad_feats, flat, flat, coef_all.reshape(halves * basis_rows, LANES))
    return output, grad_feats, grad_bases, grad_self.T, grad_coef.T


def body(
    feats,
    self_weight,
    bases,
    coef,
    src_part,
    src_row,
    edge_dst,
    edge_rel,
    block_owner,
    block_valid,
    cotangent,
):
    return layer(
        feats,
        self_weight.T,
        bases,
        coef.T,
        src_part.reshape(1, -1),
        src_row.reshape(1, -1),
        edge_dst.reshape(1, -1),
        edge_rel.reshape(1, -1),
        cotangent,
        block_owner.reshape(1, -1),
        block_valid,
        lax.axis_size(DOM),
        lax.axis_size(FEAT),
    )


def solution(mesh):
    return jax.shard_map(
        body,
        mesh=mesh,
        in_specs=(
            P(FEAT, DOM),
            P(None, FEAT),
            P(None, FEAT, None),
            P(),
            P(DOM, None),
            P(DOM),
            P(DOM),
            P(DOM),
            P(DOM, None),
            P(DOM, None),
            P(FEAT, DOM),
        ),
        out_specs=(P(FEAT, DOM), P(FEAT, DOM), P(None, FEAT, None), P(None, FEAT), P()),
        check_vma=False,
    )
```

time: 153 us -> 87.1 us (0.57); the launches traced: 150 us -> 86.2 us
  Pallas kernels: 111 us -> 85.4 us
  matrix products: 15.3 us -> 0 us
  other arithmetic: 15.1 us -> 0 us
  local copies, waits for them, and re-layouts: 7.84 us -> 0 us
    pallas_call x8 -> x2, Pallas kernels: 111 us -> 85.4 us  [the longest x1 80.7 us: layer(): pl.pallas_call(kernel, out_shape=(jax.ShapeDtypeStruct((quarter, entities...]
    dot_general x10 -> x0, matrix products: 15.3 us -> none  [dot(): lax.dot_general(left, right, (((left_axis,), (right_axis,)), ((), ())), p...]
    slice x5 -> x0, local copies, waits for them, and re-layouts: 5.4 us -> none  [the longest x1 1.89 us: body(): sources = gathered[:, :edge_count]]
    concatenate x4 -> x0, other arithmetic: 4 us -> none  [the longest x1 1.64 us: body(): jnp.concatenate([source_quarter, feats], axis=1)]
    convert_element_type x3 -> x0, other arithmetic: 3.46 us -> none  [the longest x1 1.62 us: body(): pieces = (jnp.concatenate([piece, coef_sum], axis=0) * scale).astype(BF)]
where the time goes in v1:
time: 87.1 us; the launch traced here: 86.2 us
  Pallas kernels  85.4 us (98%)
    pallas_call x1, Pallas kernels, layer(): pl.pallas_call(kernel, out_shape=(jax.ShapeDtypeStruct((quarter, entities...  80.7 us
    pallas_call x1, Pallas kernels, layer(): pl.pallas_call(last, grid=(basis_count // step,), out_shape=(jax.ShapeDty...  4.68 us

profile of v1, /device:TPU:0, one launch (start us, length us, event | category | flops | bytes accessed | tf_op | source)
XLA Modules:
  0.0 86.2 jit_solution(8819027602840240580)
XLA Ops:
  0.6 80.7 %shard_map.146 = (bf16[64,512]{1,0:T(8,128)(2,1)}, bf16[64,512]{1,0:T(8,128)(2,1)}, bf16[8,256,256]{2,1,0:T(8,128)(2,1)}, f32[8,8,128]{2,1,0:T(8,128)}) custom-call(bf16[64,512]{1,0:T(8,128)(2,1)} %feats_ref.1, bf16[64,256]{1,0:T(8,128)(2,1)} %bitcast.14, bf16[30,64,256]{2,1,0:T(8,128)(2,1)} %bases_hbm.1, f32[30,237]{1,0:T(8,128)} %bitcast.15, ...), custom_call_target="tpu_custom_call" | custom-call | tf_op jit(solution)/shard_map/pallas_call | solution.py:696
  81.4 4.7 %shard_map.147 = (bf16[64,512]{1,0:T(8,128)(2,1)}, bf16[64,512]{1,0:T(8,128)(2,1)}, f32[30,64,256]{2,1,0:T(8,128)}, f32[64,256]{1,0:T(8,128)}, f32[30,237]{1,0:T(8,128)}) custom-call(bf16[64,512]{1,0:T(8,128)(2,1)} %get-tuple-element.14.output_in, bf16[64,512]{1,0:T(8,128)(2,1)} %get-tuple-element.15.feats_in, bf16[2048,256]{1,0:T(8,128)(2,1)} %bitcast.11, ...), custom_call_target="tpu_custom_call" | custom-call | tf_op jit(solution)/shard_map/pallas_call | solution.py:731

commit v2 on v1

--- a/solution.py
+++ b/solution.py
@@ -11,6 +11,9 @@
 F32 = jnp.float32
 I32 = jnp.int32
 LANES = 128
+ROUNDS = 1
+PARTS = 2
+NODE_AT = 4
 DOM, FEAT = "dom", "feat"
 
 
@@ -18,6 +21,10 @@
     return lax.dot_general(
         left, right, (((left_axis,), (right_axis,)), ((), ())), preferred_element_type=F32
     )
+
+
+def first_of(ref):
+    return lambda count: ref.at[pl.ds(0, count)]
 
 
 def each(start, stop, step):
@@ -61,35 +68,54 @@
     )
 
 
+def wait_sent(region, sent, axis, target):
+    remote(region, region, sent.at[0], sent.at[0], axis, target).wait_send()
+
+
 class Gather:
-    def __init__(self, axis, count, source, table, sems):
+    def __init__(self, axis, count, source, table, region, sems):
         self.me, self.spot, self.side, self.columns = peers(axis, count)
-        self.axis, self.source, self.table = axis, source, table
-        self.sends, self.recvs, self.pair_sends, self.pair_recvs = sems
+        self.axis, self.source, self.table, self.region = axis, source, table, region
+        self.mate = self.spot * 2 + 1 - self.side
+        self.sent, self.recvs, self.pair_recvs = sems
+
+    def near(self, hop):
+        step, top = hop - 1, self.columns - 1
+        upper = self.spot // (self.columns // 2)
+        up = step + (step - self.spot + self.columns) // self.columns
+        mirrored = top - self.spot
+        down = top - (step + (step - mirrored + self.columns) // self.columns)
+        return up + upper * (down - up)
 
     def direct(self, hop):
-        target = (self.spot + hop) % self.columns * 2 + self.side
+        target = self.near(hop)
         return remote(
             self.source,
             self.table(self.me),
-            self.sends.at[hop - 1],
-            self.recvs.at[hop - 1],
+            self.sent.at[0],
+            self.recvs.at[self.spot],
             self.axis,
-            target,
-        )
+            target * 2 + self.side,
+        )
+
+    def arrival(self, hop):
+        spot = self.near(hop)
+        block = self.table(spot * 2 + self.side)
+        return remote(block, block, self.sent.at[0], self.recvs.at[spot], self.axis, self.mate)
 
     def place(self, hop, side):
-        return (self.spot - hop + self.columns) % self.columns * 2 + side
+        other = (hop + self.columns - 1) // self.columns
+        return (self.spot + other * (self.near(hop) - self.spot)) * 2 + side
 
     def relay(self, hop, own=False):
         spot = self.table(self.place(hop, self.side))
         return remote(
             self.source if own else spot,
             spot,
-            self.pair_sends.at[hop],
-            self.pair_recvs.at[hop],
+            self.sent.at[0],
+            self.pair_recvs.at[self.place(hop, 0) // 2],
             self.axis,
-            self.spot * 2 + 1 - self.side,
+            self.mate,
         )
 
     def start(self):
@@ -97,7 +123,7 @@
         self.relay(0, True).start()
 
     def forward(self, hop):
-        self.direct(hop).wait_recv()
+        self.arrival(hop).wait_recv()
         self.relay(hop).start()
         return self.place(hop, self.side)
 
@@ -106,28 +132,28 @@
         return self.place(hop, 1 - self.side)
 
     def finish(self):
-        each(1, self.columns, lambda hop: self.direct(hop).wait_send())
-        each(0, self.columns, lambda hop: self.relay(hop).wait_send())
+        wait_sent(self.region(2 * self.columns - 1), self.sent, self.axis, self.mate)
 
 
 def gather_sems(count):
     columns = count // 2
-    return [columns - 1, columns - 1, columns, columns]
+    return [1, columns, columns]
 
 
 class Swap:
-    def __init__(self, axis, count, source, table, sems):
+    def __init__(self, axis, count, source, table, region, sems):
         self.me = lax.axis_index(axis)
         self.axis, self.count, self.source, self.table = axis, count, source, table
-        self.sends, self.recvs = sems
+        self.region, self.together = region, sems[1].shape[0] == 1
+        self.sent, self.recvs = sems
 
     def copy(self, hop):
         target = (self.me + hop) % self.count
         return remote(
             self.source(target),
             self.table(self.me),
-            self.sends.at[hop - 1],
-            self.recvs.at[hop - 1],
+            self.sent.at[0],
+            self.recvs.at[0 if self.together else hop - 1],
             self.axis,
             target,
         )
@@ -139,20 +165,26 @@
         self.copy(hop).wait_recv()
         return (self.me - hop + self.count) % self.count
 
+    def wait_all(self):
+        region = self.region(self.count - 1)
+        other = (self.me + 1) % self.count
+        remote(region, region, self.sent.at[0], self.recvs.at[0], self.axis, other).wait_recv()
+
     def finish(self):
-        each(1, self.count, lambda hop: self.copy(hop).wait_send())
-
-
-def swap_sems(count):
-    return [count - 1, count - 1]
+        other = (self.me + 1) % self.count
+        wait_sent(self.region(self.count - 1), self.sent, self.axis, other)
+
+
+def swap_sems(count, together=True):
+    return [1, 1 if together else count - 1]
 
 
 class Reduce:
-    def __init__(self, axis, count, block, landed, summed, arrived, sems):
+    def __init__(self, axis, count, block, region, landed, summed, arrived, sems):
         self.me, self.spot, self.side, self.columns = peers(axis, count)
-        self.axis, self.block = axis, block
+        self.axis, self.block, self.region = axis, block, region
         self.landed, self.summed, self.arrived = landed, summed, arrived
-        self.sends, self.recvs, self.pair_sends, self.pair_recvs = sems
+        self.sent, self.recvs, self.pair_recvs = sems
 
     def place(self, step):
         return (self.spot + 1 + step) % self.columns
@@ -161,7 +193,7 @@
         return remote(
             self.block(self.place(step) * 2 + 1 - self.side),
             self.landed.at[step],
-            self.pair_sends.at[step],
+            self.sent.at[0],
             self.pair_recvs.at[step],
             self.axis,
             self.spot * 2 + 1 - self.side,
@@ -171,7 +203,7 @@
         return remote(
             self.summed.at[step],
             self.arrived.at[step],
-            self.sends.at[step],
+            self.sent.at[0],
             self.recvs.at[step],
             self.axis,
             self.place(step) * 2 + self.side,
@@ -196,8 +228,8 @@
         each(0, self.columns - 1, add)
 
     def drain(self):
-        each(0, self.columns, lambda step: self.passing(step).wait_send())
-        each(0, self.columns - 1, lambda step: self.onward(step).wait_send())
+        mate = self.spot * 2 + 1 - self.side
+        wait_sent(self.region(2 * self.columns - 1), self.sent, self.axis, mate)
 
 
 def sem_list(counts):
@@ -235,6 +267,9 @@
     basis_pad = total_rows // quarter
     rotated = height % quarter == 0
     group = height // quarter if rotated else group_of(basis_pad)
+    rounds = ROUNDS if rotated and group % ROUNDS == 0 else 1
+    bunch = group // rounds
+    tall = height // rounds
     basis_rows = -(-basis_count // 8) * 8
     while basis_rows * rel_pad // LANES % dom:
         basis_rows += 8
@@ -267,7 +302,7 @@
     room.messages = pltpu.VMEM((blocks, quarter, rows), BF)
     room.message_out = pltpu.VMEM((dom, cap, quarter, rows), BF)
     room.message_in = pltpu.VMEM((dom, cap, quarter, rows), BF)
-    room.message_sems = sem_list(swap_sems(dom))
+    room.message_sems = sem_list(swap_sems(dom, False))
     room.preact = pltpu.VMEM((quarter, entities), F32)
     room.aggregate = pltpu.VMEM((quarter, entities), F32)
     room.grad_out = pltpu.VMEM((dom, cap, quarter, rows), BF)
@@ -279,12 +314,13 @@
     room.self_reduce = reduce_room(feat, (quarter, entities))
     room.self_sum = pltpu.VMEM((quarter, entities), F32)
     room.stack = pltpu.VMEM((total_rows, width), BF)
-    room.stack_reduce = reduce_room(dom, (height, width))
+    room.stack_reduce = [reduce_room(dom, (tall, width)) for part in range(rounds)]
     room.piece = pltpu.VMEM((height, width), F32)
-    room.pieces_sems = sem_list(gather_sems(dom))
+    parts = PARTS if height % (16 * PARTS) == 0 else 1
+    strip = height // parts
+    room.pieces_sems = [sem_list(gather_sems(dom)) for part in range(parts)]
     room.scaled = pltpu.VMEM((basis_rows, edges), F32)
-    room.combined = pltpu.VMEM(((2 if rotated else 1) * group * quarter, edges), BF)
-    room.edge_sum = pltpu.VMEM((width, edges), F32)
+    room.combined = pltpu.VMEM((total_rows, edges), BF)
     room.edge_send = pltpu.VMEM((feat, quarter, edges), BF)
     room.edge_reduce = reduce_room(feat, (quarter, edges))
     room.edge_total = pltpu.VMEM((quarter, edges), F32)
@@ -321,9 +357,9 @@
     ):
         at = SimpleNamespace(**jax.tree.unflatten(tree, scratch))
 
-        def reduce_of(space, axis, count, block):
+        def reduce_of(space, axis, count, block, region):
             buffers, sems = space
-            return Reduce(axis, count, block, *buffers, sems)
+            return Reduce(axis, count, block, region, *buffers, sems)
 
         me = lax.axis_index(DOM)
         fme = lax.axis_index(FEAT)
@@ -386,13 +422,14 @@
         met()
 
         table = Gather(
-            DOM, dom, feats_ref, lambda place: at.table.at[place], at.table_sems
+            DOM, dom, feats_ref, lambda place: at.table.at[place], first_of(at.table), at.table_sems
         )
         slot = Swap(
             DOM,
             dom,
             lambda place: at.slot_out.at[place],
             lambda place: at.slot_in.at[place],
+            first_of(at.slot_in),
             at.slot_sems,
         )
         slot.start()
@@ -402,6 +439,7 @@
             feat,
             at.own.at[fme],
             lambda place: at.own.at[place],
+            first_of(at.own),
             at.own_sems,
         )
         own.start()
@@ -430,6 +468,7 @@
                 feat,
                 at.sources.at[fme, :, lanes],
                 lambda place, lanes=lanes: at.sources.at[place, :, lanes],
+                lambda count, lanes=lanes: at.sources.at[pl.ds(0, count), :, lanes],
                 at.source_sems[chunk],
             )
             gather.start()
@@ -462,6 +501,7 @@
             dom,
             lambda place: at.message_out.at[place],
             lambda place: at.message_in.at[place],
+            first_of(at.message_in),
             at.message_sems,
         )
 
@@ -492,7 +532,8 @@
 
         at.degree[...] = jnp.zeros((16, entities), F32)
         slot_hot(me)
-        each(1, dom, lambda hop: slot_hot(slot.wait(hop)))
+        slot.wait_all()
+        each(1, dom, lambda hop: slot_hot((me + hop) % dom))
 
         def gather_in(place):
             parts = [at.message_in[place, j] for j in range(cap)]
@@ -518,6 +559,7 @@
             dom,
             lambda place: at.grad_out.at[place],
             lambda place: at.grad_in.at[pl.ds(place * cap, cap)],
+            lambda count: at.grad_in.at[pl.ds(0, count * cap)],
             at.grad_sems,
         )
 
@@ -539,156 +581,191 @@
         at.self_send[...] = (
             dot(weight_ref[...], grad_pre, 0, 0).astype(BF).reshape(feat, quarter, entities)
         )
-        self_reduce = reduce_of(at.self_reduce, FEAT, feat, lambda place: at.self_send.at[place])
+        self_reduce = reduce_of(at.self_reduce, FEAT, feat, lambda place: at.self_send.at[place], first_of(at.self_send))
         each(0, self_reduce.columns, lambda step: self_reduce.passing(step).start())
-        at.edge_sum[...] = jnp.zeros((width, edges), F32)
-
-        each(1, dom, lambda hop: back.wait(hop))
+
+        back.wait_all()
         for k in range(blocks):
             at.grad_message[:, k * rows:(k + 1) * rows] = at.grad_in[spots[k]]
 
-        def combine(base, half):
+        deep = bunch * quarter
+
+        def combine(base):
+            start = pl.multiple_of(base * quarter, deep)
             for chunk in range(chunks):
                 lanes = pl.ds(chunk * span, span)
                 grad = at.grad_message[:, lanes].astype(F32)
-                for k in range(group):
+                for k in range(bunch):
                     weight = at.weights[pl.ds(base + k, 1), lanes]
-                    top = (half * group + k) * quarter
-                    at.combined[top:top + quarter, lanes] = (grad * weight).astype(BF)
-            block = at.combined[half * group * quarter:(half + 1) * group * quarter, :]
+                    spot = pl.ds(start + k * quarter, quarter)
+                    at.combined[spot, lanes] = (grad * weight).astype(BF)
+            block = at.combined[pl.ds(start, deep), :]
             piece = dot(block, at.sources[...].reshape(width, edges), 1, 1)
-            start = pl.multiple_of(base * quarter, group * quarter)
-            at.stack[pl.ds(start, group * quarter), :] = piece.astype(BF)
-
-            @pl.when(base + group == basis_pad)
+            at.stack[pl.ds(start, deep), :] = piece.astype(BF)
+
+            @pl.when(base + bunch == basis_pad)
             def _():
                 at.stack[cut:cut + quarter, :] = at.self_rows[...]
 
-        def part_of(base):
-            return at.bases[pl.ds(base, group)].reshape(group * quarter, width)
-
-        def edge_add(parts):
-            count = len(parts) * group * quarter
-            value = jnp.concatenate(parts, axis=0)
-            at.edge_sum[...] += dot(value, at.combined[:count, :], 0, 0)
-
-        stack = reduce_of(
-            at.stack_reduce,
-            DOM,
-            dom,
-            lambda place: at.stack.at[pl.ds(pl.multiple_of(place * height, height), height)],
-        )
+        def stack_of(part):
+            def block(place):
+                return at.stack.at[pl.ds(pl.multiple_of(place * height + part * tall, tall), tall)]
+
+            def region(count):
+                return at.stack.at[pl.ds(0, count * tall)]
+
+            return reduce_of(at.stack_reduce[part], DOM, dom, block, region)
+
+        stacks = [stack_of(part) for part in range(rounds)]
+        last_step = stacks[0].columns - 1
+        def coef_start():
+            at.scaled[...] = jnp.zeros((basis_rows, edges), F32)
+            for chunk in range(chunks):
+                lanes = pl.ds(chunk * span, span)
+                grad = at.grad_message[:, lanes].astype(F32)
+                for k in range(basis_count):
+                    value = at.products[k * quarter:(k + 1) * quarter, lanes].astype(F32) * grad
+                    at.scaled[k:k + 1, lanes] = jnp.sum(value, axis=0, keepdims=True)
+            scaled = at.scaled[...]
+            high = scaled.astype(BF)
+            low = (scaled - high.astype(F32)).astype(BF)
+            both = dot(jnp.concatenate([high, low], axis=0), at.rel_hot[...], 1, 1)
+            coef_part = (both[:basis_rows] + both[basis_rows:]) * scale
+            stacked = jnp.concatenate(
+                [coef_part[:, k * LANES:(k + 1) * LANES] for k in range(rel_pad // LANES)], axis=0
+            )
+            at.coef_out[...] = stacked.reshape(dom, coef_rows, LANES)
+            coef = Swap(
+                DOM,
+                dom,
+                lambda place: at.coef_out.at[place],
+                lambda place: at.coef_in.at[place],
+                first_of(at.coef_in),
+            at.coef_sems,
+            )
+            coef.start()
+            at.coef_in[me] = at.coef_out[me]
+            return coef
+
         if rotated:
 
             def work(step):
+                stack = stacks[part]
                 place = stack.place(step)
-                other = (place * 2 + 1 - stack.side) * group
-                mine = (place * 2 + stack.side) * group
-                combine(other, 0)
+                other = (place * 2 + 1 - stack.side) * group + part * bunch
+                mine = (place * 2 + stack.side) * group + part * bunch
+                combine(other)
                 stack.passing(step).start()
-                combine(mine, 1)
-                edge_add([part_of(other), part_of(mine)])
-
-            each(0, stack.columns, work)
+                combine(mine)
+
+            part = 0
+            work(0)
+            coef = coef_start()
+            each(1, last_step + 1, work)
+            for part in range(1, rounds):
+                each(0, last_step + 1, work)
         else:
 
             def whole(index, carry):
-                combine(index * group, 0)
-                edge_add([part_of(index * group)])
+                combine(index * bunch)
                 return carry
 
-            lax.fori_loop(0, basis_pad // group, whole, 0)
-            each(0, stack.columns, lambda step: stack.passing(step).start())
-
-        edge = reduce_of(at.edge_reduce, FEAT, feat, lambda place: at.edge_send.at[place])
-        at.edge_send[...] = at.edge_sum[...].astype(BF).reshape(feat, quarter, edges)
+            coef = coef_start()
+            lax.fori_loop(0, basis_pad // bunch, whole, 0)
+            each(0, last_step + 1, lambda step: stacks[0].passing(step).start())
+
+        edge = reduce_of(at.edge_reduce, FEAT, feat, lambda place: at.edge_send.at[place], first_of(at.edge_send))
+        every = at.bases[...].reshape(total_rows, width)
+        edge_sum = dot(every, at.combined[...], 0, 0).astype(BF)
+        at.edge_send[...] = edge_sum.reshape(feat, quarter, edges)
         each(0, edge.columns, lambda step: edge.passing(step).start())
         each(0, self_reduce.columns - 1, self_reduce.middle)
-        ahead = min(1, stack.columns - 1)
-        each(0, ahead, stack.middle)
+        soon = min(2, last_step)
+        each(0, soon, stacks[0].middle)
         each(0, edge.columns - 1, edge.middle)
-
-        at.scaled[...] = jnp.zeros((basis_rows, edges), F32)
-        for chunk in range(chunks):
-            lanes = pl.ds(chunk * span, span)
-            grad = at.grad_message[:, lanes].astype(F32)
-            for k in range(basis_count):
-                value = at.products[k * quarter:(k + 1) * quarter, lanes].astype(F32) * grad
-                at.scaled[k:k + 1, lanes] = jnp.sum(value, axis=0, keepdims=True)
-        scaled = at.scaled[...]
-        high = scaled.astype(BF)
-        low = (scaled - high.astype(F32)).astype(BF)
-        both = dot(jnp.concatenate([high, low], axis=0), at.rel_hot[...], 1, 1)
-        coef_part = (both[:basis_rows] + both[basis_rows:]) * scale
-        tall = jnp.concatenate(
-            [coef_part[:, k * LANES:(k + 1) * LANES] for k in range(rel_pad // LANES)], axis=0
-        )
-        at.coef_out[...] = tall.reshape(dom, coef_rows, LANES)
-        coef = Swap(
-            DOM,
-            dom,
-            lambda place: at.coef_out.at[place],
-            lambda place: at.coef_in.at[place],
-            at.coef_sems,
-        )
-        coef.start()
-        at.coef_in[me] = at.coef_out[me]
-        each(ahead, stack.columns - 1, stack.middle)
-
-        self_reduce.finish(at.self_sum)
-        edge.finish(at.edge_total)
-        at.edge_grad[...] = at.edge_total[...].astype(BF)
-        node = reduce_of(at.node_reduce, DOM, dom, lambda place: at.nodes.at[place])
-
-        def scatter(place):
-            at.nodes[place] = dot(at.edge_grad[...], hot_of(place), 1, 1).astype(BF)
-
-        def spread(step):
-            place = node.place(step)
-            scatter(place * 2 + 1 - node.side)
-            node.passing(step).start()
-            scatter(place * 2 + node.side)
-
-        half = node.columns // 2
-        each(0, half, spread)
-        each(1, dom, lambda hop: coef.wait(hop))
+        each(soon, last_step, stacks[0].middle)
+
+        coef.wait_all()
         at.coef_feat[fme] = jnp.sum(at.coef_in[...], axis=0)
         coef_feat = Swap(
             FEAT,
             feat,
             lambda place: at.coef_feat.at[fme],
             lambda place: at.coef_feat.at[place],
+            first_of(at.coef_feat),
             at.coef_feat_sems,
         )
         coef_feat.start()
-        each(half, node.columns, spread)
-        each(1, feat, lambda hop: coef_feat.wait(hop))
+        for stack in stacks[1:]:
+            each(0, soon, stack.middle)
+
+        self_reduce.finish(at.self_sum)
+        edge.finish(at.edge_total)
+        at.edge_grad[...] = at.edge_total[...].astype(BF)
+        node = reduce_of(at.node_reduce, DOM, dom, lambda place: at.nodes.at[place], first_of(at.nodes))
+
+        def scatter(place):
+            at.nodes[place] = dot(at.edge_grad[...], hot_of(place), 1, 1).astype(BF)
+
+        def spread(step):
+            place = node.place(step)
+            scatter(place * 2 + 1 - node.side)
+            node.passing(step).start()
+            scatter(place * 2 + node.side)
+
+        def piece_of(part):
+            rows_of = pl.ds(part * strip, strip)
+            return Gather(
+                DOM,
+                dom,
+                pieces_ref.at[me, rows_of],
+                lambda place: pieces_ref.at[place, rows_of],
+                lambda count: pieces_ref.at[pl.ds(0, count), rows_of],
+                at.pieces_sems[part],
+            )
+
+        pieces = [piece_of(part) for part in range(parts)]
+
+        def piece_send(hop):
+            for piece in pieces:
+                piece.direct(hop).start()
+
+        def piece_pass(hop):
+            for piece in pieces:
+                piece.forward(hop)
+
+        for stack in stacks[1:]:
+            each(soon, last_step, stack.middle)
+        coef_feat.wait_all()
         coef_all_ref[me] = jnp.sum(at.coef_feat[...], axis=0)
         coef_all = Swap(
             DOM,
             dom,
             lambda place: coef_all_ref.at[me],
             lambda place: coef_all_ref.at[place],
+            first_of(coef_all_ref),
             at.coef_all_sems,
         )
         coef_all.start()
-
-        stack.finish(at.piece)
+        each(0, node.columns, spread)
+        stacks[0].finish(at.piece)
         pieces_ref[me] = (at.piece[...] * scale).astype(BF)
-        pieces = Gather(
-            DOM, dom, pieces_ref.at[me], lambda place: pieces_ref.at[place], at.pieces_sems
-        )
-        pieces.start()
+        each(1, node.columns, piece_send)
+        for piece in pieces:
+            piece.relay(0, True).start()
+        held = min(NODE_AT, node.columns)
+        each(1, held, piece_pass)
         each(0, node.columns - 1, node.middle)
-        each(1, pieces.columns, lambda hop: pieces.forward(hop))
+        each(held, node.columns, piece_pass)
         node.finish(at.node_sum)
         grad_feats_ref[...] = (at.self_sum[...] + at.node_sum[...]).astype(BF)
-        each(0, pieces.columns, lambda hop: pieces.from_mate(hop))
-        each(1, dom, lambda hop: coef_all.wait(hop))
-
-        for done in [table, slot, own, message, back, coef, coef_feat, coef_all, pieces] + gathers:
+        for piece in pieces:
+            each(0, piece.columns, lambda hop: piece.from_mate(hop))
+        coef_all.wait_all()
+
+        for done in [table, slot, own, message, back, coef, coef_feat, coef_all] + gathers + pieces:
             done.finish()
-        for done in [self_reduce, stack, edge, node]:
+        for done in [self_reduce, edge, node] + stacks:
             done.drain()
 
     vmem = pl.BlockSpec(memory_space=pltpu.VMEM)
@@ -712,25 +789,26 @@
     step = group_of(basis_count)
     halves = rel_pad // LANES
 
-    def last(output_in, feats_in, bases_in, self_in, coef_in, *outs):
-        outs[2][...] = bases_in[...].astype(F32).reshape(step, quarter, width)
-
-        @pl.when(pl.program_id(0) == 0)
-        def _():
-            outs[0][...] = output_in[...]
-            outs[1][...] = feats_in[...]
-            outs[3][...] = self_in[...].astype(F32)
-            parts = [coef_in[k * basis_rows:(k + 1) * basis_rows] for k in range(halves)]
-            outs[4][...] = jnp.concatenate(parts, axis=1)[:basis_count, :relations]
-
-    flat = pieces.reshape(total_rows, width)
-
-    def fixed(shape, spot=0):
-        return pl.BlockSpec(shape, lambda index: (spot,) + (0,) * (len(shape) - 1))
+    def last(output_in, feats_in, flat_in, coef_in, *outs):
+        output_out, feats_out, bases_out, self_out, coef_out, wide, sem = outs
+        copies = []
+        for index in range(basis_count // step):
+            spots = pl.ds(index * step, step)
+            value = flat_in[index * step * quarter:(index + 1) * step * quarter, :]
+            wide[spots] = value.astype(F32).reshape(step, quarter, width)
+            copy = pltpu.make_async_copy(wide.at[spots], bases_out.at[spots], sem.at[index])
+            copy.start()
+            copies.append(copy)
+        output_out[...] = output_in[...]
+        feats_out[...] = feats_in[...]
+        self_out[...] = flat_in[cut:cut + quarter, :].astype(F32)
+        parts = [coef_in[k * basis_rows:(k + 1) * basis_rows] for k in range(halves)]
+        coef_out[...] = jnp.concatenate(parts, axis=1)[:basis_count, :relations]
+        for copy in copies:
+            copy.wait()
 
     output, grad_feats, grad_bases, grad_self, grad_coef = pl.pallas_call(
         last,
-        grid=(basis_count // step,),
         out_shape=(
             jax.ShapeDtypeStruct((quarter, entities), BF),
             jax.ShapeDtypeStruct((quarter, entities), BF),
@@ -738,21 +816,18 @@
             jax.ShapeDtypeStruct((quarter, width), F32),
             jax.ShapeDtypeStruct((basis_count, relations), F32),
         ),
-        in_specs=[
-            fixed((quarter, entities)),
-            fixed((quarter, entities)),
-            pl.BlockSpec((step * quarter, width), lambda index: (index, 0)),
-            fixed((quarter, width), cut // quarter),
-            fixed((halves * basis_rows, LANES)),
+        in_specs=[vmem] * 4,
+        out_specs=(vmem, vmem, pl.BlockSpec(memory_space=pl.ANY), vmem, vmem),
+        scratch_shapes=[
+            pltpu.VMEM((basis_count, quarter, width), F32),
+            pltpu.SemaphoreType.DMA((basis_count // step,)),
         ],
-        out_specs=(
-            fixed((quarter, entities)),
-            fixed((quarter, entities)),
-            pl.BlockSpec((step, quarter, width), lambda index: (index, 0, 0)),
-            fixed((quarter, width)),
-            fixed((basis_count, relations)),
-        ),
-    )(output, grad_feats, flat, flat, coef_all.reshape(halves * basis_rows, LANES))
+    )(
+        output,
+        grad_feats,
+        pieces.reshape(total_rows, width),
+        coef_all.reshape(halves * basis_rows, LANES),
+    )
     return output, grad_feats, grad_bases, grad_self.T, grad_coef.T
 
 

time: 87.1 us -> 82.3 us (0.945)
  Pallas kernels: 85.4 us -> 81.3 us
    pallas_call x1, Pallas kernels: 80.7 us -> 78 us  [layer(): pl.pallas_call(kernel, out_shape=(jax.ShapeDtypeStruct((quarter, entities...]
    pallas_call x1, Pallas kernels: 4.68 us -> 3.32 us  [layer(): pl.pallas_call(last, out_shape=(jax.ShapeDtypeStruct((quarter, entities),...]
where the time goes in v2:
time: 82.3 us; the launch traced here: 82.1 us
  Pallas kernels  81.3 us (99%)
    pallas_call x1, Pallas kernels, layer(): pl.pallas_call(kernel, out_shape=(jax.ShapeDtypeStruct((quarter, entities...  78 us
    pallas_call x1, Pallas kernels, layer(): pl.pallas_call(last, out_shape=(jax.ShapeDtypeStruct((quarter, entities),...  3.32 us

profile of v2, /device:TPU:0, one launch (start us, length us, event | category | flops | bytes accessed | tf_op | source)
XLA Modules:
  0.0 82.1 jit_solution(10302710409588433155)
XLA Ops:
  0.6 78.0 %shard_map.146 = (bf16[64,512]{1,0:T(8,128)(2,1)}, bf16[64,512]{1,0:T(8,128)(2,1)}, bf16[8,256,256]{2,1,0:T(8,128)(2,1)}, f32[8,8,128]{2,1,0:T(8,128)}) custom-call(bf16[64,512]{1,0:T(8,128)(2,1)} %feats_ref.1, bf16[64,256]{1,0:T(8,128)(2,1)} %bitcast.12, bf16[30,64,256]{2,1,0:T(8,128)(2,1)} %bases_hbm.1, f32[30,237]{1,0:T(8,128)} %bitcast.13, ...), custom_call_target="tpu_custom_call" | custom-call | tf_op jit(solution)/shard_map/pallas_call | solution.py:773
  78.6 3.3 %shard_map.147 = (bf16[64,512]{1,0:T(8,128)(2,1)}, bf16[64,512]{1,0:T(8,128)(2,1)}, f32[30,64,256]{2,1,0:T(8,128)}, f32[64,256]{1,0:T(8,128)}, f32[30,237]{1,0:T(8,128)}) custom-call(bf16[64,512]{1,0:T(8,128)(2,1)} %get-tuple-element.14.output_in, bf16[64,512]{1,0:T(8,128)(2,1)} %get-tuple-element.15.feats_in, bf16[2048,256]{1,0:T(8,128)(2,1)} %bitcast.11, ...), custom_call_target="tpu_custom_call" | custom-call | tf_op jit(solution)/shard_map/pallas_call | solution.py:810

commit v3 on v2

--- a/solution.py
+++ b/solution.py
@@ -12,8 +12,7 @@
 I32 = jnp.int32
 LANES = 128
 ROUNDS = 1
-PARTS = 2
-NODE_AT = 4
+PARTS = 4
 DOM, FEAT = "dom", "feat"
 
 
@@ -138,6 +137,83 @@
 def gather_sems(count):
     columns = count // 2
     return [1, columns, columns]
+
+
+class Chain:
+    def __init__(self, axis, count, table, region, sems):
+        self.me, self.spot, self.side, self.columns = peers(axis, count)
+        self.axis, self.table, self.region = axis, table, region
+        self.mate = self.spot * 2 + 1 - self.side
+        self.sent, self.moved, self.recvs, self.pair_recvs = sems
+
+    def step(self, spot, way):
+        block = self.table(spot * 2 + self.side)
+        upper = (way + 1) // 2
+        return remote(
+            block,
+            block,
+            self.moved.at[upper * self.columns + spot],
+            self.recvs.at[spot],
+            self.axis,
+            (self.spot + way) * 2 + self.side,
+        )
+
+    def relay(self, spot, side):
+        block = self.table(spot * 2 + side)
+        return remote(
+            block, block, self.sent.at[0], self.pair_recvs.at[spot], self.axis, self.mate
+        )
+
+    def can(self, way):
+        return self.spot < self.columns - 1 if way > 0 else self.spot > 0
+
+    def start(self):
+        for way in (1, -1):
+
+            @pl.when(self.can(way))
+            def _():
+                self.step(self.spot, way).start()
+
+        self.relay(self.spot, self.side).start()
+
+    def holds(self, spot):
+        return jnp.logical_and(spot >= 0, spot < self.columns)
+
+    def forward(self, hop):
+        for way in (1, -1):
+            spot = self.spot - way * hop
+
+            @pl.when(self.holds(spot))
+            def _():
+                copy = self.step(spot, way)
+                copy.wait_recv()
+
+                @pl.when(self.can(way))
+                def _():
+                    copy.start()
+
+                self.relay(spot, self.side).start()
+
+    def from_mate(self, spot):
+        self.relay(spot, 1 - self.side).wait_recv()
+
+    def finish(self):
+        wait_sent(self.region(self.columns), self.sent, self.axis, self.mate)
+
+        def drain(hop):
+            for way in (1, -1):
+                spot = self.spot - way * hop
+
+                @pl.when(jnp.logical_and(self.holds(spot), self.can(way)))
+                def _():
+                    self.step(spot, way).wait_send()
+
+        each(0, self.columns, drain)
+
+
+def chain_sems(count):
+    columns = count // 2
+    return [1, 2 * columns, columns, columns]
 
 
 class Swap:
@@ -318,7 +394,7 @@
     room.piece = pltpu.VMEM((height, width), F32)
     parts = PARTS if height % (16 * PARTS) == 0 else 1
     strip = height // parts
-    room.pieces_sems = [sem_list(gather_sems(dom)) for part in range(parts)]
+    room.pieces_sems = [sem_list(chain_sems(dom)) for part in range(parts)]
     room.scaled = pltpu.VMEM((basis_rows, edges), F32)
     room.combined = pltpu.VMEM((total_rows, edges), BF)
     room.edge_send = pltpu.VMEM((feat, quarter, edges), BF)
@@ -715,20 +791,15 @@
 
         def piece_of(part):
             rows_of = pl.ds(part * strip, strip)
-            return Gather(
+            return Chain(
                 DOM,
                 dom,
-                pieces_ref.at[me, rows_of],
                 lambda place: pieces_ref.at[place, rows_of],
                 lambda count: pieces_ref.at[pl.ds(0, count), rows_of],
                 at.pieces_sems[part],
             )
 
         pieces = [piece_of(part) for part in range(parts)]
-
-        def piece_send(hop):
-            for piece in pieces:
-                piece.direct(hop).start()
 
         def piece_pass(hop):
             for piece in pieces:
@@ -750,13 +821,10 @@
         each(0, node.columns, spread)
         stacks[0].finish(at.piece)
         pieces_ref[me] = (at.piece[...] * scale).astype(BF)
-        each(1, node.columns, piece_send)
         for piece in pieces:
-            piece.relay(0, True).start()
-        held = min(NODE_AT, node.columns)
-        each(1, held, piece_pass)
+            piece.start()
+        each(1, node.columns, piece_pass)
         each(0, node.columns - 1, node.middle)
-        each(held, node.columns, piece_pass)
         node.finish(at.node_sum)
         grad_feats_ref[...] = (at.self_sum[...] + at.node_sum[...]).astype(BF)
         for piece in pieces:

time: 82.3 us -> 80.6 us (0.979)
  Pallas kernels: 81.3 us -> 79.6 us
    pallas_call x1, Pallas kernels: 78 us -> 76.3 us  [layer(): pl.pallas_call(kernel, out_shape=(jax.ShapeDtypeStruct((quarter, entities...]
where the time goes in v3:
time: 80.6 us; the launch traced here: 80.4 us
  Pallas kernels  79.6 us (99%)
    pallas_call x1, Pallas kernels, layer(): pl.pallas_call(kernel, out_shape=(jax.ShapeDtypeStruct((quarter, entities...  76.3 us
    pallas_call x1, Pallas kernels, layer(): pl.pallas_call(last, out_shape=(jax.ShapeDtypeStruct((quarter, entities),...  3.32 us

profile of v3, /device:TPU:0, one launch (start us, length us, event | category | flops | bytes accessed | tf_op | source)
XLA Modules:
  0.0 80.4 jit_solution(9453332290867032518)
XLA Ops:
  0.6 76.3 %shard_map.146 = (bf16[64,512]{1,0:T(8,128)(2,1)}, bf16[64,512]{1,0:T(8,128)(2,1)}, bf16[8,256,256]{2,1,0:T(8,128)(2,1)}, f32[8,8,128]{2,1,0:T(8,128)}) custom-call(bf16[64,512]{1,0:T(8,128)(2,1)} %feats_ref.1, bf16[64,256]{1,0:T(8,128)(2,1)} %bitcast.12, bf16[30,64,256]{2,1,0:T(8,128)(2,1)} %bases_hbm.1, f32[30,237]{1,0:T(8,128)} %bitcast.13, ...), custom_call_target="tpu_custom_call" | custom-call | tf_op jit(solution)/shard_map/pallas_call | solution.py:841
  76.9 3.3 %shard_map.147 = (bf16[64,512]{1,0:T(8,128)(2,1)}, bf16[64,512]{1,0:T(8,128)(2,1)}, f32[30,64,256]{2,1,0:T(8,128)}, f32[64,256]{1,0:T(8,128)}, f32[30,237]{1,0:T(8,128)}) custom-call(bf16[64,512]{1,0:T(8,128)(2,1)} %get-tuple-element.14.output_in, bf16[64,512]{1,0:T(8,128)(2,1)} %get-tuple-element.15.feats_in, bf16[2048,256]{1,0:T(8,128)(2,1)} %bitcast.11, ...), custom_call_target="tpu_custom_call" | custom-call | tf_op jit(solution)/shard_map/pallas_call | solution.py:878

commit v4 on v3

--- a/solution.py
+++ b/solution.py
@@ -356,7 +356,10 @@
 
     room = SimpleNamespace()
     room.bases = pltpu.VMEM((basis_pad, quarter, width), BF)
-    room.bases_sems = sem_list([1])
+    given = (feats, weight_t, coef_t, part, row, dst, rel, cotangent)
+    room.given = [pltpu.VMEM(value.shape, value.dtype) for value in given]
+    room.counts = [pltpu.SMEM(value.shape, value.dtype) for value in (owner, valid)]
+    room.load_sems = sem_list([3 + len(given)])
     room.weights = pltpu.VMEM((basis_pad, edges), F32)
     room.rel_hot = pltpu.VMEM((rel_pad, edges), BF)
     room.coef_wide = pltpu.VMEM((basis_rows, rel_pad), F32)
@@ -368,7 +371,9 @@
     room.hots = pltpu.VMEM((dom, entities, slots), BF)
     room.degree = pltpu.VMEM((16, entities), F32)
     room.table = pltpu.VMEM((dom, quarter, entities), BF)
-    room.table_sems = sem_list(gather_sems(dom))
+    bands = 2 if quarter % 32 == 0 else 1
+    band = quarter // bands
+    room.table_sems = [sem_list(gather_sems(dom)) for part in range(bands)]
     room.picked = pltpu.VMEM((quarter, edges), F32)
     room.own = pltpu.VMEM((feat, quarter, entities), BF)
     room.own_sems = sem_list(gather_sems(feat))
@@ -414,17 +419,17 @@
     shapes, tree = jax.tree.flatten(vars(room))
 
     def kernel(
-        feats_ref,
-        weight_ref,
         bases_hbm,
-        coef_ref,
-        part_ref,
-        row_ref,
-        dst_ref,
-        rel_ref,
-        cot_ref,
-        owner_ref,
-        valid_ref,
+        feats_hbm,
+        weight_hbm,
+        coef_hbm,
+        part_hbm,
+        row_hbm,
+        dst_hbm,
+        rel_hbm,
+        cot_hbm,
+        owner_hbm,
+        valid_hbm,
         output_ref,
         grad_feats_ref,
         pieces_ref,
@@ -441,13 +446,32 @@
         fme = lax.axis_index(FEAT)
         met = greet([(DOM, dom), (FEAT, feat)])
 
-        load = pltpu.make_async_copy(
-            bases_hbm, at.bases.at[pl.ds(0, basis_count)], at.bases_sems[0].at[0]
-        )
-        load.start()
+        feats_ref, weight_ref, coef_ref, part_ref, row_ref, dst_ref, rel_ref, cot_ref = at.given
+        owner_ref, valid_ref = at.counts
+        pairs = [
+            (feats_hbm, feats_ref),
+            (weight_hbm, weight_ref),
+            (coef_hbm, coef_ref),
+            (part_hbm, part_ref),
+            (row_hbm, row_ref),
+            (dst_hbm, dst_ref),
+            (rel_hbm, rel_ref),
+            (cot_hbm, cot_ref),
+            (owner_hbm, owner_ref),
+            (valid_hbm, valid_ref),
+            (bases_hbm, at.bases.at[pl.ds(0, basis_count)]),
+        ]
+        loads = [
+            pltpu.make_async_copy(source, target, at.load_sems[0].at[index])
+            for index, (source, target) in enumerate(pairs)
+        ]
+        for load in loads:
+            load.start()
         if basis_pad > basis_count:
             extra = basis_pad - basis_count
             at.bases[basis_count:] = jnp.zeros((extra, quarter, width), BF)
+        for load in loads[:-1]:
+            load.wait()
         at.sids[...] = part_ref[...] * entities + row_ref[...]
         lane = lax.broadcasted_iota(I32, (1, rows), 1)
         spots = []
@@ -497,9 +521,25 @@
 
         met()
 
-        table = Gather(
-            DOM, dom, feats_ref, lambda place: at.table.at[place], first_of(at.table), at.table_sems
-        )
+        def table_of(part):
+            rows_of = pl.ds(part * band, band)
+            return Gather(
+                DOM,
+                dom,
+                feats_ref.at[rows_of],
+                lambda place: at.table.at[place, rows_of],
+                lambda count: at.table.at[pl.ds(0, count), rows_of],
+                at.table_sems[part],
+            )
+
+        tables = [table_of(part) for part in range(bands)]
+
+        def table_pass(hop):
+            return [table.forward(hop) for table in tables][0]
+
+        def table_take(hop):
+            return [table.from_mate(hop) for table in tables][0]
+
         slot = Swap(
             DOM,
             dom,
@@ -509,7 +549,9 @@
             at.slot_sems,
         )
         slot.start()
-        table.start()
+        each(1, tables[0].columns, lambda hop: [table.direct(hop).start() for table in tables])
+        for table in tables:
+            table.relay(0, True).start()
         own = Gather(
             FEAT,
             feat,
@@ -530,10 +572,10 @@
             at.picked[...] += dot(at.table[place], hot_of(place), 1, 0)
 
         at.picked[...] = dot(feats_ref[...], hot_of(me), 1, 0)
-        use(table.from_mate(0))
+        use(table_take(0))
         each(1, own.columns, lambda hop: own.forward(hop))
-        each(1, table.columns, lambda hop: use(table.forward(hop)))
-        each(1, table.columns, lambda hop: use(table.from_mate(hop)))
+        each(1, tables[0].columns, lambda hop: use(table_pass(hop)))
+        each(1, tables[0].columns, lambda hop: use(table_take(hop)))
 
         gathers = []
         for chunk in range(chunks):
@@ -552,7 +594,7 @@
         each(0, own.columns, lambda hop: own.from_mate(hop))
         own_full = at.own[...].reshape(width, entities)
         at.preact[...] = dot(weight_ref[...], own_full, 1, 0)
-        load.wait()
+        loads[-1].wait()
 
         def forward(chunk):
             lanes = pl.ds(chunk * span, span)
@@ -831,13 +873,13 @@
             each(0, piece.columns, lambda hop: piece.from_mate(hop))
         coef_all.wait_all()
 
-        for done in [table, slot, own, message, back, coef, coef_feat, coef_all] + gathers + pieces:
+        exchanges = [slot, own, message, back, coef, coef_feat, coef_all]
+        for done in tables + exchanges + gathers + pieces:
             done.finish()
         for done in [self_reduce, edge, node] + stacks:
             done.drain()
 
     vmem = pl.BlockSpec(memory_space=pltpu.VMEM)
-    smem = pl.BlockSpec(memory_space=pltpu.SMEM)
     output, grad_feats, pieces, coef_all = pl.pallas_call(
         kernel,
         out_shape=(
@@ -846,13 +888,13 @@
             jax.ShapeDtypeStruct((dom, height, width), BF),
             jax.ShapeDtypeStruct((dom, coef_rows, LANES), F32),
         ),
-        in_specs=[vmem, vmem, pl.BlockSpec(memory_space=pl.ANY)] + [vmem] * 6 + [smem] * 2,
+        in_specs=[pl.BlockSpec(memory_space=pltpu.HBM)] * 11,
         out_specs=(vmem,) * 4,
         scratch_shapes=shapes,
         compiler_params=pltpu.CompilerParams(
             collective_id=0, has_side_effects=True, vmem_limit_bytes=60 * 1024 * 1024
         ),
-    )(feats, weight_t, bases, coef_t, part, row, dst, rel, cotangent, owner, valid)
+    )(bases, *given, owner, valid)
 
     step = group_of(basis_count)
     halves = rel_pad // LANES

time: 80.6 us -> 79.2 us (0.983)
  Pallas kernels: 79.6 us -> 78.3 us
    pallas_call x1, Pallas kernels: 76.3 us -> 75 us  [layer(): pl.pallas_call(kernel, out_shape=(jax.ShapeDtypeStruct((quarter, entities...]
where the time goes in v4:
time: 79.2 us; the launch traced here: 79.1 us
  Pallas kernels  78.3 us (99%)
  between operations  0.8 us (1%)
    pallas_call x1, Pallas kernels, layer(): pl.pallas_call(kernel, out_shape=(jax.ShapeDtypeStruct((quarter, entities...  75 us
    pallas_call x1, Pallas kernels, layer(): pl.pallas_call(last, out_shape=(jax.ShapeDtypeStruct((quarter, entities),...  3.32 us

profile of v4, /device:TPU:0, one launch (start us, length us, event | category | flops | bytes accessed | tf_op | source)
XLA Modules:
  0.0 79.1 jit_solution(2363791241567442388)
XLA Ops:
  0.6 75.0 %shard_map.146 = (bf16[64,512]{1,0:T(8,128)(2,1)}, bf16[64,512]{1,0:T(8,128)(2,1)}, bf16[8,256,256]{2,1,0:T(8,128)(2,1)}, f32[8,8,128]{2,1,0:T(8,128)}) custom-call(bf16[30,64,256]{2,1,0:T(8,128)(2,1)} %bases_hbm.1, bf16[64,512]{1,0:T(8,128)(2,1)} %feats_hbm.1, bf16[64,256]{1,0:T(8,128)(2,1)} %bitcast.12, f32[30,237]{1,0:T(8,128)} %bitcast.13, ...), custom_call_target="tpu_custom_call" | custom-call | tf_op jit(solution)/shard_map/pallas_call | solution.py:883
  75.6 3.3 %shard_map.147 = (bf16[64,512]{1,0:T(8,128)(2,1)}, bf16[64,512]{1,0:T(8,128)(2,1)}, f32[30,64,256]{2,1,0:T(8,128)}, f32[64,256]{1,0:T(8,128)}, f32[30,237]{1,0:T(8,128)}) custom-call(bf16[64,512]{1,0:T(8,128)(2,1)} %get-tuple-element.14.output_in, bf16[64,512]{1,0:T(8,128)(2,1)} %get-tuple-element.15.feats_in, bf16[2048,256]{1,0:T(8,128)(2,1)} %bitcast.11, ...), custom_call_target="tpu_custom_call" | custom-call | tf_op jit(solution)/shard_map/pallas_call | solution.py:920
